TPU v7x, 32 devices: a whole 2x2x4 slice. The times are simulated.
32 devices in a mesh: wide: 8 (over z, core), narrow: 4 (over y, x).
Axes of the slice: x: 2, y: 2, z: 4, core: 2. Of those that a mesh axis runs over, the one named last changes fastest.
Arguments:
- activations: bfloat16 [512, 16384], P(None, 'wide'), may hold values from -6 to 6
- enc_weight: bfloat16 [16384, 4096], P('wide', 'narrow'), may hold values from -0.046875 to 0.046875
- enc_bias: float32 [4096], P('narrow'), may hold values from -4 to 4
- dec_weight: bfloat16 [4096, 16384], P('narrow', 'wide'), may hold values from -0.375 to 0.375
- dec_bias: float32 [16384], P('wide'), may hold values from -4 to 4
- active_ids: int32 [512, 64], replicated, may hold values from 0 to 4095, all different within a row
Outputs:
- dec_grad: bfloat16 [4096, 16384], P('narrow', 'wide')
- latent_grad: float32 [512, 4096], P('wide', 'narrow')
Inputs may be any that keep to these rules, and one draw needn't show every extreme that they name: `active_ids`: each row names 64 different latents; every latent is named by some row.
All inputs are finite; a program needn't handle non-finite values.
Results may differ from a plain program's by a relative error of at most 0.0058.
Values may be sent and summed in bfloat16 or wider, within the bound.
A program may use at most 128 MiB of HBM per device.

v0:
```python
import functools

import jax
import jax.numpy as jnp
from jax import lax
from jax.experimental import pallas as pl
from jax.experimental.pallas import tpu as pltpu
from jax.sharding import PartitionSpec as P

LANES = 128
SUBLANES = 8
MESH = pl.DeviceIdType.MESH


def lookup(table, index):
    return jnp.take_along_axis(table, index, axis=1, mode="promise_in_bounds")


def pick_active(dense_ref, ids, first_row, rows, fold, top):
    tile, lane = ids >> 7, ids & (LANES - 1)
    half = lax.broadcasted_iota(jnp.int32, ids.shape, 1) // top
    picked = jnp.zeros(ids.shape, jnp.float32)
    for part in range(fold):
        here = jnp.where(half == part, tile, -1)
        for j in range(dense_ref.shape[1] // LANES):
            start = first_row + part * rows
            table = dense_ref[pl.ds(start, rows), j * LANES : (j + 1) * LANES]
            picked = jnp.where(here == j, lookup(table, lane), picked)
    return picked


def encode_kernel(steps, fold, top, act_ref, enc_ref, bias_ref, ids_ref, out_ref, total):
    step = pl.program_id(0)
    product = jnp.dot(act_ref[...], enc_ref[...], preferred_element_type=jnp.float32)

    @pl.when(step == 0)
    def _():
        first = (lax.axis_index("wide") == 0).astype(jnp.float32)
        total[...] = product + first * bias_ref[...]

    @pl.when(step > 0)
    def _():
        total[...] += product

    @pl.when(step == steps - 1)
    def _():
        blocks, rows = ids_ref.shape[:2]
        low = lax.axis_index("narrow") * total.shape[1]

        def block(w, carry):
            start = pl.multiple_of(w * (rows * fold), rows)
            out_ref[w] = pick_active(total, ids_ref[w] - low, start, rows, fold, top)
            return carry

        lax.fori_loop(0, blocks, block, 0)


def main_kernel(
    W, N, fold, top, chunk,
    part_ref, ids_ref, packed_ids_ref, bias_ref, act_hbm, dec_hbm,
    lat_ref, err_hbm, grad_ref,
    act, dec, slot, wide_in, values, rec, rec_in, err_out, err, lg, lg_packed, grad_in,
    load_sem, out_sem, ws1, wr1, ws2, wr2, ws3, wr3, ns1, nr1, ns2, nr2,
):
    wide, narrow = lax.axis_index("wide"), lax.axis_index("narrow")
    tokens, latents = lat_ref.shape
    own, rows = tokens // N, part_ref.shape[1]
    chunks = err.shape[1] // chunk
    load_act = pltpu.make_async_copy(
        act_hbm.at[pl.ds(pl.multiple_of(narrow * own, own), own)], act, load_sem.at[0]
    )
    load_dec = pltpu.make_async_copy(dec_hbm, dec, load_sem.at[1])
    load_act.start()
    load_dec.start()

    barrier = pltpu.get_barrier_semaphore()
    for d in range(1, W):
        pl.semaphore_signal(barrier, inc=1, device_id={"wide": lax.rem(wide + d, W)}, device_id_type=MESH)
    for d in range(1, N):
        pl.semaphore_signal(barrier, inc=1, device_id={"narrow": lax.rem(narrow + d, N)}, device_id_type=MESH)
    pl.semaphore_wait(barrier, W + N - 2)

    def wide_copy(d, source, target, send, recv):
        return pltpu.make_async_remote_copy(
            src_ref=source, dst_ref=target, send_sem=send.at[d], recv_sem=recv.at[d],
            device_id={"wide": lax.rem(wide + d, W)}, device_id_type=MESH,
        )

    def scatter_copy(d, source, target, send, recv):
        return wide_copy(d, source.at[lax.rem(wide + d, W)], target.at[d], send, recv)

    for d in range(1, W):
        scatter_copy(d, part_ref, wide_in, ws1, wr1).start()

    low = narrow * latents

    def slots_of(i, carry):
        at = pl.ds(pl.multiple_of(i * SUBLANES, SUBLANES), SUBLANES)
        ids = ids_ref[at, :] - low
        place = lax.broadcasted_iota(jnp.int32, (SUBLANES, latents), 1)
        found = jnp.full((SUBLANES, latents), -1, jnp.int32)
        for k in range(top):
            found = jnp.where(ids[:, k : k + 1] == place, k, found)
        slot[at, :] = found
        return carry

    groups = tokens // SUBLANES
    lax.fori_loop(0, groups // 2, slots_of, 0)

    total = part_ref[wide]
    for d in range(1, W):
        scatter_copy(d, part_ref, wide_in, ws1, wr1).wait_recv()
        total = total + wide_in[d]
    values[wide] = total
    for d in range(1, W):
        wide_copy(d, values.at[wide], values.at[wide], ws2, wr2).start()

    lax.fori_loop(groups // 2, groups, slots_of, 0)
    for d in range(1, W):
        wide_copy(d, values.at[wide], values.at[wide], ws2, wr2).wait_recv()

    def spread(table, block, part):
        at = pl.ds(pl.multiple_of((block * fold + part) * rows, rows), rows)
        pieces = []
        for j in range(latents // LANES):
            index = slot[at, j * LANES : (j + 1) * LANES]
            found = lookup(table, jnp.maximum(index, 0) + part * top)
            pieces.append(jnp.where(index >= 0, found, 0.0))
        return jnp.concatenate(pieces, axis=1)

    def fill(block, carry):
        table = values[block]
        both = jnp.concatenate([spread(table, block, part) for part in range(fold)], axis=0)
        at = pl.ds(pl.multiple_of(block * (fold * rows), fold * rows), fold * rows)
        lat_ref[at, :] = both.astype(jnp.bfloat16)
        return carry

    lax.fori_loop(0, W, fill, 0)
    load_act.wait()
    load_dec.wait()

    def narrow_copy(d, source, target, send, recv):
        return pltpu.make_async_remote_copy(
            src_ref=source, dst_ref=target, send_sem=send, recv_sem=recv,
            device_id={"narrow": lax.rem(narrow + d, N)}, device_id_type=MESH,
        )

    def rec_copy(c, d):
        return narrow_copy(d, rec.at[c, lax.rem(narrow + d, N)], rec_in.at[c, d], ns1.at[c, d], nr1.at[c, d])

    def columns(c):
        return pl.ds(pl.multiple_of(c * chunk, chunk), chunk)

    def own_rows(i):
        return pl.ds(pl.multiple_of(i * own, own), own)

    def err_copy(c, d):
        return narrow_copy(d, err_out.at[c, d], err.at[own_rows(narrow), columns(c)], ns2.at[c, d], nr2.at[c, d])

    def decode(c, carry):
        product = jnp.dot(lat_ref[...], dec[:, columns(c)], preferred_element_type=jnp.float32)
        rec[c] = product.astype(jnp.bfloat16).reshape(N, own, chunk)
        for d in range(1, N):
            rec_copy(c, d).start()
        return carry

    lax.fori_loop(0, chunks, decode, 0)

    def combine(c, carry):
        for d in range(1, N):
            rec_copy(c, d).wait_recv()
        shift = bias_ref[:, columns(c)] - act[:, columns(c)].astype(jnp.float32)
        terms = [rec[c, narrow].astype(jnp.float32)]
        terms += [rec_in[c, d].astype(jnp.float32) for d in range(1, N)]
        for e in range(N):
            goal = lax.rem(narrow + e, N)
            back = (N - goal).astype(jnp.float32) * shift
            for d in range(N):
                origin = lax.rem(narrow + N - d, N)
                back = back + (N - jnp.maximum(goal, origin)).astype(jnp.float32) * terms[d]
            back = (back / N).astype(jnp.bfloat16)
            if e == 0:
                err[own_rows(narrow), columns(c)] = back
            else:
                err_out[c, e] = back
                err_copy(c, e).start()
        return carry

    lax.fori_loop(0, chunks, combine, 0)

    def out_copy(c):
        return pltpu.make_async_copy(err.at[:, columns(c)], err_hbm.at[:, columns(c)], out_sem.at[c])

    def contract(c):
        for d in range(1, N):
            err_copy(c, d).wait_recv()
        out_copy(c).start()
        return lax.dot_general(
            err[:, columns(c)], dec[:, columns(c)], (((1,), (1,)), ((), ())), preferred_element_type=jnp.float32
        )

    lg[...] = contract(0)

    def more(c, carry):
        lg[...] += contract(c)
        return carry

    lax.fori_loop(1, chunks, more, 0)

    def pack(w, carry):
        start = pl.multiple_of(w * (rows * fold), rows)
        lg_packed[w] = pick_active(lg, packed_ids_ref[w] - low, start, rows, fold, top)
        return carry

    lax.fori_loop(0, W, pack, 0)
    for d in range(1, W):
        scatter_copy(d, lg_packed, grad_in, ws3, wr3).start()
    total = lg_packed[wide]
    for d in range(1, W):
        scatter_copy(d, lg_packed, grad_in, ws3, wr3).wait_recv()
        total = total + grad_in[d]
    for part in range(fold):
        grad_ref[part * rows : (part + 1) * rows, :] = spread(total, wide, part)

    for d in range(1, W):
        scatter_copy(d, part_ref, wide_in, ws1, wr1).wait_send()
        wide_copy(d, values.at[wide], values.at[wide], ws2, wr2).wait_send()
        scatter_copy(d, lg_packed, grad_in, ws3, wr3).wait_send()

    def drain(c, carry):
        for d in range(1, N):
            rec_copy(c, d).wait_send()
            err_copy(c, d).wait_send()
        out_copy(c).wait()
        return carry

    lax.fori_loop(0, chunks, drain, 0)


def local(activations, enc_weight, enc_bias, dec_weight, dec_bias, active_ids):
    W, N = lax.axis_size("wide"), lax.axis_size("narrow")
    tokens, channels = activations.shape
    latents = enc_weight.shape[1]
    top = active_ids.shape[1]
    fold = max(1, LANES // top)
    rows = tokens // W // fold
    packed_ids = (
        active_ids.reshape(W, fold, rows, top).transpose(0, 2, 1, 3).reshape(W, rows, fold * top)
    )
    depth = min(channels, 512)
    steps = channels // depth
    f32, bf16 = jnp.float32, jnp.bfloat16
    vmem = pl.BlockSpec(memory_space=pltpu.VMEM)
    hbm = pl.BlockSpec(memory_space=pl.ANY)
    flops = 2 * tokens * channels * latents
    packed = pl.pallas_call(
        functools.partial(encode_kernel, steps, fold, top),
        grid=(steps,),
        out_shape=jax.ShapeDtypeStruct((W, rows, fold * top), f32),
        in_specs=[
            pl.BlockSpec((tokens, depth), lambda k: (0, k)),
            pl.BlockSpec((depth, latents), lambda k: (k, 0)),
            pl.BlockSpec((1, latents), lambda k: (0, 0)),
            pl.BlockSpec((W, rows, fold * top), lambda k: (0, 0, 0)),
        ],
        out_specs=pl.BlockSpec((W, rows, fold * top), lambda k: (0, 0, 0)),
        scratch_shapes=[pltpu.VMEM((tokens, latents), f32)],
        cost_estimate=pl.CostEstimate(flops=flops, bytes_accessed=2 * channels * (tokens + latents), transcendentals=0),
        name="encode",
    )(activations, enc_weight, enc_bias.reshape(1, -1), packed_ids)

    chunk = min(channels, 256)
    chunks = channels // chunk
    own = tokens // N
    packed_shape = (W, rows, fold * top)
    dma = pltpu.SemaphoreType.DMA
    lat, err, latent_grad = pl.pallas_call(
        functools.partial(main_kernel, W, N, fold, top, chunk),
        out_shape=(
            jax.ShapeDtypeStruct((tokens, latents), bf16),
            jax.ShapeDtypeStruct((tokens, channels), bf16),
            jax.ShapeDtypeStruct((tokens // W, latents), f32),
        ),
        in_specs=[vmem, vmem, vmem, vmem, hbm, hbm],
        out_specs=(vmem, hbm, vmem),
        scratch_shapes=[
            pltpu.VMEM((own, channels), bf16),
            pltpu.VMEM((latents, channels), bf16),
            pltpu.VMEM((tokens, latents), jnp.int32),
            pltpu.VMEM(packed_shape, f32),
            pltpu.VMEM(packed_shape, f32),
            pltpu.VMEM((chunks, N, own, chunk), bf16),
            pltpu.VMEM((chunks, N, own, chunk), bf16),
            pltpu.VMEM((chunks, N, own, chunk), bf16),
            pltpu.VMEM((tokens, channels), bf16),
            pltpu.VMEM((tokens, latents), f32),
            pltpu.VMEM(packed_shape, f32),
            pltpu.VMEM(packed_shape, f32),
            dma((2,)), dma((chunks,)),
            dma((W,)), dma((W,)), dma((W,)), dma((W,)), dma((W,)), dma((W,)),
            dma((chunks, N)), dma((chunks, N)), dma((chunks, N)), dma((chunks, N)),
        ],
        compiler_params=pltpu.CompilerParams(collective_id=0, has_side_effects=True, vmem_limit_bytes=56 * 2**20),
        cost_estimate=pl.CostEstimate(flops=2 * flops, bytes_accessed=2 * channels * (2 * tokens + latents), transcendentals=0),
        name="exchange",
    )(packed, active_ids, packed_ids, dec_bias.reshape(1, -1), activations, dec_weight)
    dec_grad = lax.dot_general(lat, err, (((0,), (0,)), ((), ())), preferred_element_type=f32).astype(bf16)
    return dec_grad, latent_grad


def solution(mesh):
    in_specs = (
        P(None, "wide"),
        P("wide", "narrow"),
        P("narrow"),
        P("narrow", "wide"),
        P("wide"),
        P(),
    )
    out_specs = (P("narrow", "wide"), P("wide", "narrow"))
    return jax.shard_map(local, mesh=mesh, in_specs=in_specs, out_specs=out_specs, check_vma=False)
```

profile of v0, /device:TPU:0, one launch (start us, length us, event | category | flops | bytes accessed | tf_op | source)
XLA Modules:
  0.0 96.1 jit_solution(10513410992310970412)
XLA Ops:
  0.6 1.0 %copy.10.ids_ref = s32[512,64]{1,0:T(8,128)S(1)} copy(s32[512,64]{0,1:T(8,128)} %param.11) | data formatting | bytes 262144 | tf_op args[5]
  1.7 0.0 copy-start
  1.7 0.2 copy.11
  1.9 0.8 reshape.18.ids_ref.packed_ids_ref
  2.7 8.3 %encode.1.part_ref = f32[8,32,128]{2,1,0:T(8,128)} custom-call(bf16[512,2048]{1,0:T(8,128)(2,1)} %act_hbm.1, bf16[2048,1024]{1,0:T(8,128)(2,1)} %enc_ref.1, f32[1,1024]{1,0:T(1,128)} %bitcast.9, s32[8,32,128]{2,1,0:T(8,128)} %reshape.18.ids_ref.packed_ids_ref), custom_call_target="tpu_custom_call" | custom-call | flops 2147483648 | bytes 6291456 | tf_op jit(solution)/shard_map/encode/pallas_call | solution.py:256
  11.0 0.0 copy-done
  11.0 78.0 %exchange.1 = (bf16[512,1024]{1,0:T(8,128)(2,1)}, bf16[512,2048]{1,0:T(8,128)(2,1)}, f32[64,1024]{1,0:T(8,128)}) custom-call(f32[8,32,128]{2,1,0:T(8,128)} %encode.1.part_ref, s32[512,64]{1,0:T(8,128)} %copy-done, s32[8,32,128]{2,1,0:T(8,128)} %reshape.18.ids_ref.packed_ids_ref, f32[1,2048]{1,0:T(1,128)} %bitcast.8, bf16[512,2048]{1,0:T(8,128)(2,1)} %act_hbm.1, ...), custom_call_target="tpu_custom_call" | custom-call | flops 4294967296 | bytes 8388608 | tf_op jit(solution)/shard_map/exchange/pallas_call | solution.py:277
  89.0 0.0 copy-start.1
  89.0 6.4 %convolution_convert_fusion = bf16[1024,2048]{1,0:T(8,128)(2,1)} fusion(bf16[512,1024]{1,0:T(8,128)(2,1)} %get-tuple-element.5, bf16[512,2048]{1,0:T(8,128)(2,1)} %get-tuple-element.6), kind=kOutput, calls=%fused_computation | convolution fusion | flops 2149580800 | bytes 7340032 | tf_op jit(solution)/shard_map/dot_general | solution.py:307
  95.4 0.0 copy-done.1
  95.4 0.7 copy.14
Async XLA Ops:
  1.7 9.3 %copy-start = (s32[512,64]{1,0:T(8,128)}, s32[512,64]{1,0:T(8,128)S(1)}, u32[]{:S(2)}) copy-start(s32[512,64]{1,0:T(8,128)S(1)} %copy.10.ids_ref) | copy-start | bytes 393220
  89.0 6.4 %copy-start.1 = (f32[64,1024]{1,0:T(8,128)S(1)}, f32[64,1024]{1,0:T(8,128)}, u32[]{:S(2)}) copy-start(f32[64,1024]{1,0:T(8,128)} %get-tuple-element.11) | copy-start | bytes 786436
where the time goes:
time: 96.3 us; the launch traced here: 96.1 us
  Pallas kernels  86.3 us (90%)
  matrix products  6.35 us (7%)
  local copies, waits for them, and re-layouts  2.78 us (3%)
    pallas_call x1, Pallas kernels, local(): pl.pallas_call(functools.partial(main_kernel, W, N, fold, top, chunk), ou...  78 us
    pallas_call x1, Pallas kernels, local(): pl.pallas_call(functools.partial(encode_kernel, steps, fold, top), grid=(...  8.27 us
    dot_general x1, matrix products, local(): lax.dot_general(lat, err, (((0,), (0,)), ((), ())), preferred_element_typ...  6.35 us

commit v1 on v0

v1 whole, which is shorter than its diff:
```python
import functools

import jax
import jax.numpy as jnp
from jax import lax
from jax.experimental import pallas as pl
from jax.experimental.pallas import tpu as pltpu
from jax.sharding import PartitionSpec as P

LANES = 128
MESH = pl.DeviceIdType.MESH
F32, BF16 = jnp.float32, jnp.bfloat16


def lookup(table, index):
    return jnp.take_along_axis(table, index, axis=1, mode="promise_in_bounds")


def pick(tables, ids, fold, top):
    tile, lane = ids >> 7, ids & (LANES - 1)
    half = lax.broadcasted_iota(jnp.int32, ids.shape, 1) // top
    picked = jnp.zeros(ids.shape, F32)
    for part in range(fold):
        here = jnp.where(half == part, tile, -1)
        for j, table in enumerate(tables(part)):
            picked = jnp.where(here == j, lookup(table, lane), picked)
    return picked


def step_kernel(
    W, N, fold, top, chunk, pieces,
    ids_t_ref, bias_ref, shift_ref, act_hbm, enc_hbm, dec_hbm,
    dg_ref, grad_ref,
    ids, act, enc, dec, slot, total, mine, part, wide_in, values, lat, lat_t,
    rec, rec_in, err_out, err, lg_packed, grad_in,
    load_sem, ws1, wr1, ws2, wr2, ws3, wr3, ns1, nr1, ns2, nr2,
):
    wide, narrow = lax.axis_index("wide"), lax.axis_index("narrow")
    tokens, latents = lat.shape
    channels = act.shape[1]
    own, rows = tokens // N, part.shape[1]
    chunks = channels // chunk
    piece = latents // pieces
    low = narrow * latents

    def piece_cols(n):
        return pl.ds(pl.multiple_of(n * piece, LANES), piece)

    load_act = pltpu.make_async_copy(act_hbm, act, load_sem.at[0])
    load_dec = pltpu.make_async_copy(dec_hbm, dec, load_sem.at[1])

    def load_enc(n):
        return pltpu.make_async_copy(enc_hbm.at[:, piece_cols(n)], enc.at[:, piece_cols(n)], load_sem.at[2 + n])

    load_act.start()
    for n in range(pieces):
        load_enc(n).start()
    load_dec.start()

    barrier = pltpu.get_barrier_semaphore()
    for d in range(1, W):
        pl.semaphore_signal(barrier, inc=1, device_id={"wide": lax.rem(wide + d, W)}, device_id_type=MESH)
    for d in range(1, N):
        pl.semaphore_signal(barrier, inc=1, device_id={"narrow": lax.rem(narrow + d, N)}, device_id_type=MESH)

    stacked = jnp.concatenate([ids_t_ref[...]] * fold, axis=0) - low
    ids[...] = stacked.T

    GROUP = 16
    groups = tokens // GROUP

    def slots_of(i, carry):
        at = pl.ds(pl.multiple_of(i * GROUP, GROUP), GROUP)
        mine_ids = ids[at, :]
        place = lax.broadcasted_iota(jnp.int32, (GROUP, LANES), 1)
        places = [(place + j * LANES).astype(jnp.int16) for j in range(latents // LANES)]
        found = [jnp.full((GROUP, LANES), -1, jnp.int16) for _ in places]
        for k in range(top):
            here = jnp.broadcast_to(mine_ids[:, k : k + 1], (GROUP, LANES)).astype(jnp.int16)
            found = [jnp.where(here == p, jnp.int16(k), f) for p, f in zip(places, found)]
        for j, f in enumerate(found):
            slot[at, j * LANES : (j + 1) * LANES] = f
        return carry

    lax.fori_loop(0, groups // 4, slots_of, 0)

    load_act.wait()

    def encode(n, carry):
        pltpu.make_async_copy(enc_hbm.at[:, piece_cols(n)], enc.at[:, piece_cols(n)], load_sem.at[2 + n]).wait()
        total[:, piece_cols(n)] = jnp.dot(act[...], enc[:, piece_cols(n)], preferred_element_type=F32)
        return carry

    lax.fori_loop(0, pieces, encode, 0)

    half = lax.broadcasted_iota(jnp.int32, (rows, LANES), 1) // top

    def packed_ids(w):
        out = ids[pl.ds(pl.multiple_of(w * (rows * fold), rows), rows), :]
        for p in range(1, fold):
            other = ids[pl.ds(pl.multiple_of((w * fold + p) * rows, rows), rows), :]
            out = jnp.where(half == p, other, out)
        return out

    def pick_dense(w):
        def tables(p):
            at = pl.ds(pl.multiple_of((w * fold + p) * rows, rows), rows)
            return [total[at, j * LANES : (j + 1) * LANES] for j in range(latents // LANES)]

        return pick(tables, packed_ids(w), fold, top)

    def pick_block(w, carry):
        picked = pick_dense(w)
        mine[w] = picked
        part[w] = picked.astype(BF16)
        return carry

    lax.fori_loop(0, W, pick_block, 0)

    pl.semaphore_wait(barrier, W + N - 2)

    def wide_copy(d, source, target, send, recv):
        return pltpu.make_async_remote_copy(
            src_ref=source, dst_ref=target, send_sem=send.at[d], recv_sem=recv.at[d],
            device_id={"wide": lax.rem(wide + d, W)}, device_id_type=MESH,
        )

    def scatter_copy(d, source, target, send, recv):
        return wide_copy(d, source.at[lax.rem(wide + d, W)], target.at[d], send, recv)

    for d in range(1, W):
        scatter_copy(d, part, wide_in, ws1, wr1).start()

    def bias_tables(p):
        return [jnp.broadcast_to(bias_ref[:, j * LANES : (j + 1) * LANES], (rows, LANES)) for j in range(latents // LANES)]

    summed = mine[wide] + pick(bias_tables, packed_ids(wide), fold, top)

    lax.fori_loop(groups // 4, groups * 5 // 8, slots_of, 0)

    for d in range(1, W):
        scatter_copy(d, part, wide_in, ws1, wr1).wait_recv()
        summed = summed + wide_in[d].astype(F32)
    values[wide] = summed.astype(BF16)
    for d in range(1, W):
        wide_copy(d, values.at[wide], values.at[wide], ws2, wr2).start()

    lax.fori_loop(groups * 5 // 8, groups, slots_of, 0)
    for d in range(1, W):
        wide_copy(d, values.at[wide], values.at[wide], ws2, wr2).wait_recv()

    def spread(table, block, p):
        at = pl.ds(pl.multiple_of((block * fold + p) * rows, rows), rows)
        out = []
        for j in range(latents // LANES):
            index = slot[at, j * LANES : (j + 1) * LANES].astype(jnp.int32)
            found = lookup(table, jnp.maximum(index, 0) + p * top)
            out.append(jnp.where(index >= 0, found, 0.0))
        return jnp.concatenate(out, axis=1)

    def fill(block, carry):
        table = values[block].astype(F32)
        both = jnp.concatenate([spread(table, block, p) for p in range(fold)], axis=0)
        at = pl.ds(pl.multiple_of(block * (fold * rows), fold * rows), fold * rows)
        lat[at, :] = both.astype(BF16)
        return carry

    lax.fori_loop(0, W, fill, 0)
    load_dec.wait()

    def narrow_copy(d, source, target, send, recv):
        return pltpu.make_async_remote_copy(
            src_ref=source, dst_ref=target, send_sem=send, recv_sem=recv,
            device_id={"narrow": lax.rem(narrow + d, N)}, device_id_type=MESH,
        )

    def rec_copy(c, d):
        return narrow_copy(d, rec.at[c, lax.rem(narrow + d, N)], rec_in.at[c, d], ns1.at[c, d], nr1.at[c, d])

    def columns(c):
        return pl.ds(pl.multiple_of(c * chunk, chunk), chunk)

    def own_rows(i):
        return pl.ds(pl.multiple_of(i * own, own), own)

    def err_copy(c, d):
        return narrow_copy(d, err_out.at[c, d], err.at[own_rows(narrow), columns(c)], ns2.at[c, d], nr2.at[c, d])

    def decode(c, carry):
        product = jnp.dot(lat[...], dec[:, columns(c)], preferred_element_type=F32)
        rec[c] = product.astype(BF16).reshape(N, own, chunk)
        for d in range(1, N):
            rec_copy(c, d).start()
        return carry

    lax.fori_loop(0, chunks, decode, 0)

    def flip(j, carry):
        at = pl.ds(pl.multiple_of(j * LANES, LANES), LANES)
        lat_t[at, :] = lat[:, at].T
        return carry

    def combine(c, carry):
        for d in range(1, N):
            rec_copy(c, d).wait_recv()
        shift = shift_ref[:, columns(c)] - act[own_rows(narrow), columns(c)].astype(F32)
        terms = [rec[c, narrow].astype(F32)]
        terms += [rec_in[c, d].astype(F32) for d in range(1, N)]
        for e in range(N):
            goal = lax.rem(narrow + e, N)
            back = (N - goal).astype(F32) * shift
            for d in range(N):
                origin = lax.rem(narrow + N - d, N)
                back = back + (N - jnp.maximum(goal, origin)).astype(F32) * terms[d]
            back = (back / N).astype(BF16)
            if e == 0:
                err[own_rows(narrow), columns(c)] = back
            else:
                err_out[c, e] = back
                err_copy(c, e).start()
        return carry

    lax.fori_loop(0, chunks, combine, 0)
    lax.fori_loop(0, latents // LANES, flip, 0)

    def contract(c):
        for d in range(1, N):
            err_copy(c, d).wait_recv()
        return lax.dot_general(
            err[:, columns(c)], dec[:, columns(c)], (((1,), (1,)), ((), ())), preferred_element_type=F32
        )

    def outer(c):
        dg_ref[:, columns(c)] = jnp.dot(lat_t[...], err[:, columns(c)], preferred_element_type=F32).astype(BF16)

    total[...] = contract(0)

    def more(c, carry):
        outer(c - 1)
        total[...] += contract(c)
        return carry

    lax.fori_loop(1, chunks, more, 0)

    def pack(w, carry):
        picked = pick_dense(w)
        mine[w] = picked
        lg_packed[w] = picked.astype(BF16)
        return carry

    lax.fori_loop(0, W, pack, 0)
    for d in range(1, W):
        scatter_copy(d, lg_packed, grad_in, ws3, wr3).start()
    outer(chunks - 1)
    summed = mine[wide]
    for d in range(1, W):
        scatter_copy(d, lg_packed, grad_in, ws3, wr3).wait_recv()
        summed = summed + grad_in[d].astype(F32)
    for p in range(fold):
        grad_ref[p * rows : (p + 1) * rows, :] = spread(summed, wide, p)

    for d in range(1, W):
        scatter_copy(d, part, wide_in, ws1, wr1).wait_send()
        wide_copy(d, values.at[wide], values.at[wide], ws2, wr2).wait_send()
        scatter_copy(d, lg_packed, grad_in, ws3, wr3).wait_send()

    def drain(c, carry):
        for d in range(1, N):
            rec_copy(c, d).wait_send()
            err_copy(c, d).wait_send()
        return carry

    lax.fori_loop(0, chunks, drain, 0)


def local(activations, enc_weight, enc_bias, dec_weight, dec_bias, active_ids):
    W, N = lax.axis_size("wide"), lax.axis_size("narrow")
    tokens, channels = activations.shape
    latents = enc_weight.shape[1]
    top = active_ids.shape[1]
    fold = LANES // top
    rows = tokens // W // fold
    chunk = min(channels, 256)
    chunks = channels // chunk
    pieces = 4
    own = tokens // N
    packed_shape = (W, rows, LANES)
    vmem = pl.BlockSpec(memory_space=pltpu.VMEM)
    hbm = pl.BlockSpec(memory_space=pl.ANY)
    dma = pltpu.SemaphoreType.DMA
    dec_grad, latent_grad = pl.pallas_call(
        functools.partial(step_kernel, W, N, fold, top, chunk, pieces),
        out_shape=(
            pltpu.VMEM((latents, channels), BF16),
            pltpu.VMEM((tokens // W, latents), F32),
        ),
        in_specs=[vmem, vmem, vmem, hbm, hbm, hbm],
        out_specs=(vmem, vmem),
        scratch_shapes=[
            pltpu.VMEM((tokens, LANES), jnp.int32),
            pltpu.VMEM((tokens, channels), BF16),
            pltpu.VMEM((channels, latents), BF16),
            pltpu.VMEM((latents, channels), BF16),
            pltpu.VMEM((tokens, latents), jnp.int16),
            pltpu.VMEM((tokens, latents), F32),
            pltpu.VMEM(packed_shape, F32),
            pltpu.VMEM(packed_shape, BF16),
            pltpu.VMEM(packed_shape, BF16),
            pltpu.VMEM(packed_shape, BF16),
            pltpu.VMEM((tokens, latents), BF16),
            pltpu.VMEM((latents, tokens), BF16),
            pltpu.VMEM((chunks, N, own, chunk), BF16),
            pltpu.VMEM((chunks, N, own, chunk), BF16),
            pltpu.VMEM((chunks, N, own, chunk), BF16),
            pltpu.VMEM((tokens, channels), BF16),
            pltpu.VMEM(packed_shape, BF16),
            pltpu.VMEM(packed_shape, BF16),
            dma((2 + pieces,)),
            dma((W,)), dma((W,)), dma((W,)), dma((W,)), dma((W,)), dma((W,)),
            dma((chunks, N)), dma((chunks, N)), dma((chunks, N)), dma((chunks, N)),
        ],
        compiler_params=pltpu.CompilerParams(collective_id=0, has_side_effects=True, vmem_limit_bytes=56 * 2**20),
        cost_estimate=pl.CostEstimate(
            flops=8 * tokens * channels * latents, bytes_accessed=6 * channels * (tokens + latents), transcendentals=0
        ),
        name="step",
    )(active_ids.T, enc_bias.reshape(1, -1), dec_bias.reshape(1, -1), activations, enc_weight, dec_weight)
    return dec_grad, latent_grad


def solution(mesh):
    in_specs = (
        P(None, "wide"),
        P("wide", "narrow"),
        P("narrow"),
        P("narrow", "wide"),
        P("wide"),
        P(),
    )
    out_specs = (P("narrow", "wide"), P("wide", "narrow"))
    return jax.shard_map(local, mesh=mesh, in_specs=in_specs, out_specs=out_specs, check_vma=False)
```

time: 96.3 us -> 80.7 us (0.84)
  Pallas kernels: 86.3 us -> 77.2 us
  matrix products: 6.35 us -> 0 us
    pallas_call x2 -> x1, Pallas kernels: 86.3 us -> 77.2 us  [local(): pl.pallas_call(functools.partial(step_kernel, W, N, fold, top, chunk, pie...]
    dot_general x1 -> x0, matrix products: 6.35 us -> none  [local(): lax.dot_general(lat, err, (((0,), (0,)), ((), ())), preferred_element_typ...]
    unnamed x6 -> x2, local copies, waits for them, and re-layouts: 1.74 us -> 2.72 us
where the time goes in v1:
time: 80.7 us; the launch traced here: 80.5 us
  Pallas kernels  77.2 us (96%)
  local copies, waits for them, and re-layouts  2.72 us (3%)
    pallas_call x1, Pallas kernels, local(): pl.pallas_call(functools.partial(step_kernel, W, N, fold, top, chunk, pie...  77.2 us
    unnamed x2, local copies, waits for them, and re-layouts  2.72 us

profile of v1, /device:TPU:0, one launch (start us, length us, event | category | flops | bytes accessed | tf_op | source)
XLA Modules:
  0.0 80.5 jit_solution(10191650227012814175)
XLA Ops:
  0.6 77.2 %step.1 = (bf16[1024,2048]{1,0:T(8,128)(2,1)S(1)}, f32[64,1024]{1,0:T(8,128)S(1)}) custom-call(s32[64,512]{1,0:T(8,128)} %bitcast.3, f32[1,1024]{1,0:T(1,128)} %bitcast.5, f32[1,2048]{1,0:T(1,128)} %bitcast.4, bf16[512,2048]{1,0:T(8,128)(2,1)} %act_hbm.1, bf16[2048,1024]{1,0:T(8,128)(2,1)} %enc_hbm.1, bf16[1024,2048]{1,0:T(8,128)(2,1)} %dec_hbm.1), custom_call_target="tpu_custom_call" | custom-call | flops 8589934592 | bytes 18874368 | tf_op jit(solution)/shard_map/step/pallas_call | solution.py:291
  77.8 2.0 %copy.10 = bf16[1024,2048]{1,0:T(8,128)(2,1)} copy(bf16[1024,2048]{1,0:T(8,128)(2,1)S(1)} %get-tuple-element.2) | data formatting | bytes 8388608
  79.8 0.7 copy.11

commit v2 on v1

v2 whole, which is shorter than its diff:
```python
import functools

import jax
import jax.numpy as jnp
from jax import lax
from jax.experimental import pallas as pl
from jax.experimental.pallas import tpu as pltpu
from jax.sharding import PartitionSpec as P

LANES = 128
MESH = pl.DeviceIdType.MESH
F32, BF16 = jnp.float32, jnp.bfloat16


def lookup(table, index):
    return jnp.take_along_axis(table, index, axis=1, mode="promise_in_bounds")


def pick(tables, ids, fold, top):
    tile, lane = ids >> 7, ids & (LANES - 1)
    half = lax.broadcasted_iota(jnp.int32, ids.shape, 1) // top
    picked = jnp.zeros(ids.shape, F32)
    for part in range(fold):
        here = jnp.where(half == part, tile, -1)
        for j, table in enumerate(tables(part)):
            picked = jnp.where(here == j, lookup(table, lane), picked)
    return picked


def step_kernel(
    W, N, fold, top, chunk, pieces, early,
    ids_t_ref, bias_ref, shift_ref, act_hbm, enc_hbm, dec_hbm,
    dg_ref, grad_ref,
    ids, act, enc, dec, slot, total, mine, part, wide_in, values, lat, lat_t,
    err, lg_packed, grad_in,
    load_sem, ws1, wr1, ws2, wr2, ws3, wr3, *scratch,
):
    wide, narrow = lax.axis_index("wide"), lax.axis_index("narrow")
    tokens, latents = lat.shape
    channels = act.shape[1]
    own, rows = tokens // N, part.shape[1]
    chunks = channels // chunk
    piece = latents // pieces
    low = narrow * latents

    def piece_cols(n):
        return pl.ds(pl.multiple_of(n * piece, LANES), piece)

    load_act = pltpu.make_async_copy(act_hbm, act, load_sem.at[0])
    head = channels - early * chunk
    load_dec = pltpu.make_async_copy(dec_hbm.at[:, :head], dec.at[:, :head], load_sem.at[1])

    def load_enc(n):
        return pltpu.make_async_copy(enc_hbm.at[:, piece_cols(n)], enc.at[:, piece_cols(n)], load_sem.at[2 + n])

    if early:
        load_rest = pltpu.make_async_copy(dec_hbm.at[:, head:], dec.at[:, head:], load_sem.at[2 + pieces])
        load_rest.start()
    load_act.start()
    for n in range(pieces):
        load_enc(n).start()
    load_dec.start()

    barrier = pltpu.get_barrier_semaphore()
    for d in range(1, W):
        pl.semaphore_signal(barrier, inc=1, device_id={"wide": lax.rem(wide + d, W)}, device_id_type=MESH)
    for d in range(1, N):
        pl.semaphore_signal(barrier, inc=1, device_id={"narrow": lax.rem(narrow + d, N)}, device_id_type=MESH)

    stacked = jnp.concatenate([ids_t_ref[...]] * fold, axis=0)
    ids[...] = stacked.T

    GROUP, TALL = 16, 256
    bands = latents // TALL
    groups = bands * (tokens // LANES)

    def fill_slots(i, slot, low):
        band, side = i % bands, i // bands
        at = pl.ds(pl.multiple_of(side * LANES, LANES), LANES)
        offset = low + band * TALL
        place = lax.broadcasted_iota(jnp.int32, (GROUP, LANES), 0)
        places = [(place + j * GROUP).astype(jnp.int16) for j in range(TALL // GROUP)]
        found = [jnp.full((GROUP, LANES), top, jnp.int16) for _ in places]
        for k in range(top):
            here = jnp.broadcast_to(ids_t_ref[k : k + 1, at] - offset, (GROUP, LANES)).astype(jnp.int16)
            found = [jnp.where(here == p, jnp.int16(k), f) for p, f in zip(places, found)]
        slot[at, pl.ds(pl.multiple_of(band * TALL, TALL), TALL)] = jnp.concatenate(found, axis=0).T

    def slots_of(i, carry):
        fill_slots(i, slot, low)
        return carry

    lax.fori_loop(0, groups // 4, slots_of, 0)
    pl.semaphore_wait(barrier, W + N - 2)

    def narrow_copy(goal, source, target, send, recv):
        return pltpu.make_async_remote_copy(
            src_ref=source, dst_ref=target, send_sem=send, recv_sem=recv,
            device_id={"narrow": goal}, device_id_type=MESH,
        )

    def wide_copy(d, source, target, send, recv):
        return pltpu.make_async_remote_copy(
            src_ref=source, dst_ref=target, send_sem=send.at[d], recv_sem=recv.at[d],
            device_id={"wide": lax.rem(wide + d, W)}, device_id_type=MESH,
        )

    def columns(c):
        return pl.ds(pl.multiple_of(c * chunk, chunk), chunk)

    if early:
        (
            dec_in, slot_in, values_in, lat_in, rec, rec_in, msg, msg_in, err_out, full, full_in, base,
            ds, dr, vs, vr, vws, vwr, ns1, nr1, ns2, nr2, ns3, nr3, fs, fr,
        ) = scratch
        side, pair = lax.rem(narrow, 2), narrow // 2
        across, along = narrow + 1 - 2 * side, narrow + 2 - 4 * pair
        plain = chunks - early

        PARTS = 2
        tall = latents // PARTS

        def dec_copy(i):
            c, at = i // PARTS, pl.ds(i % PARTS * tall, tall)
            return narrow_copy(
                across, dec.at[at, columns(plain + c)], dec_in.at[at, columns(c)], ds.at[i], dr.at[i]
            )

        load_rest.wait()
        for i in range(early * PARTS - 1):
            dec_copy(i).start()
    else:
        rec, rec_in, err_out, ns1, nr1, ns2, nr2 = scratch

    load_act.wait()

    def encode(n, carry):
        pltpu.make_async_copy(enc_hbm.at[:, piece_cols(n)], enc.at[:, piece_cols(n)], load_sem.at[2 + n]).wait()
        total[:, piece_cols(n)] = jnp.dot(act[...], enc[:, piece_cols(n)], preferred_element_type=F32)
        return carry

    lax.fori_loop(0, pieces, encode, 0)

    half = lax.broadcasted_iota(jnp.int32, (rows, LANES), 1) // top

    def packed_ids(w):
        out = ids[pl.ds(w * (rows * fold), rows), :]
        for p in range(1, fold):
            other = ids[pl.ds((w * fold + p) * rows, rows), :]
            out = jnp.where(half == p, other, out)
        return out - low

    def pick_dense(w):
        def tables(p):
            at = pl.ds((w * fold + p) * rows, rows)
            return [total[at, j * LANES : (j + 1) * LANES] for j in range(latents // LANES)]

        return pick(tables, packed_ids(w), fold, top)

    def pick_block(w, carry):
        picked = pick_dense(w)
        mine[w] = picked
        part[w] = picked.astype(BF16)
        return carry

    for w in range(W):
        pick_block(w, 0)

    def scatter_copy(d, source, target, send, recv):
        return wide_copy(d, source.at[lax.rem(wide + d, W)], target.at[d], send, recv)

    for d in range(1, W):
        scatter_copy(d, part, wide_in, ws1, wr1).start()

    def bias_tables(p):
        return [jnp.broadcast_to(bias_ref[:, j * LANES : (j + 1) * LANES], (rows, LANES)) for j in range(latents // LANES)]

    summed = mine[wide] + pick(bias_tables, packed_ids(wide), fold, top)

    lax.fori_loop(groups // 4, groups * 5 // 8, slots_of, 0)

    for d in range(1, W):
        scatter_copy(d, part, wide_in, ws1, wr1).wait_recv()
        summed = summed + wide_in[d].astype(F32)
    values[wide] = summed.astype(BF16)
    for d in range(1, W):
        wide_copy(d, values.at[wide], values.at[wide], ws2, wr2).start()
    if early:
        def pair_values():
            return narrow_copy(across, values.at[wide], values_in.at[wide], vs.at[0], vr.at[0])

        pair_values().start()
        dec_copy(early * PARTS - 1).start()

    lax.fori_loop(groups * 5 // 8, groups, slots_of, 0)
    for d in range(1, W):
        wide_copy(d, values.at[wide], values.at[wide], ws2, wr2).wait_recv()

    def spread(table, slot, block, p):
        start = (block * fold + p) * rows
        at = pl.ds(start if isinstance(start, int) else pl.multiple_of(start, rows), rows)
        table = table[:, p * top : (p + 1) * top]
        table = jnp.concatenate([table, jnp.zeros((rows, LANES - top), F32)], axis=1)
        out = []
        for j in range(latents // LANES):
            out.append(lookup(table, slot[at, j * LANES : (j + 1) * LANES].astype(jnp.int32)))
        return jnp.concatenate(out, axis=1)

    def fill(values, slot, lat):
        for block in range(W):
            table = values[block].astype(F32)
            both = jnp.concatenate([spread(table, slot, block, p) for p in range(fold)], axis=0)
            lat[block * (fold * rows) : (block + 1) * (fold * rows), :] = both.astype(BF16)

    fill(values, slot, lat)
    load_dec.wait()

    def own_rows(i):
        return pl.ds(pl.multiple_of(i * own, own), own)

    def flip(j, carry):
        at = pl.ds(pl.multiple_of(j * LANES, LANES), LANES)
        lat_t[at, :] = lat[:, at].T
        return carry

    def decode(c):
        return jnp.dot(lat[...], dec[:, columns(c)], preferred_element_type=F32)

    if early:
        mates = N // 2
        share = tokens // mates
        here = pl.ds(pl.multiple_of(side * share, share), share)

        def scale(count):
            return count.astype(F32)

        own_scale, mate_scale = scale(N - narrow), scale(N - across)
        least = scale(N - jnp.maximum(narrow, across))
        own_use, mate_use = scale(1 + pair * (N - 1 - narrow)), scale(1 + pair * (N - 1 - across))

        def rec_copy(c):
            return narrow_copy(across, rec.at[c, 1 - side], rec_in.at[c], ns1.at[c], nr1.at[c])

        def msg_copy(c):
            return narrow_copy(along, msg.at[c], msg_in.at[c], ns2.at[c], nr2.at[c])

        def err_copy(c):
            return narrow_copy(across, err_out.at[c], err.at[here, columns(c)], ns3.at[c], nr3.at[c])

        def full_copy(c):
            return narrow_copy(along, full.at[c], full_in.at[c], fs.at[c], fr.at[c])

        def send_rec(c, carry):
            rec[c] = decode(c).astype(BF16).reshape(mates, share, chunk)
            rec_copy(c).start()
            return carry

        lax.fori_loop(0, plain, send_rec, 0)

        def more_slots(i, carry):
            fill_slots(i, slot_in, across * latents)
            return carry

        def send_msg(c, carry):
            rec_copy(c).wait_recv()
            msg[c] = (own_use * rec[c, side].astype(F32) + mate_use * rec_in[c].astype(F32)).astype(BF16)
            msg_copy(c).start()
            return carry

        def send_err(c, carry):
            msg_copy(c).wait_recv()
            shift = shift_ref[:, columns(c)] - act[here, columns(c)].astype(F32)
            mine_rec, mate_rec = rec[c, side].astype(F32), rec_in[c].astype(F32)
            other = msg_in[c].astype(F32)
            back = own_scale * (shift + mine_rec) + least * mate_rec + own_use * other
            err[here, columns(c)] = (back / N).astype(BF16)
            back = mate_scale * (shift + mate_rec) + least * mine_rec + mate_use * other
            err_out[c] = (back / N).astype(BF16)
            err_copy(c).start()
            return carry

        def send_full(c, carry):
            mine_rec = decode(plain + c)
            mate_rec = jnp.dot(lat_in[...], dec_in[:, columns(c)], preferred_element_type=F32)
            full[c] = (own_use * mine_rec + mate_use * mate_rec).astype(BF16)
            full_copy(c).start()
            shift = shift_ref[:, columns(plain + c)] - act[:, columns(plain + c)].astype(F32)
            base[c] = own_scale * (shift + mine_rec) + least * mate_rec
            return carry

        def take_full(c, carry):
            full_copy(c).wait_recv()
            err[:, columns(plain + c)] = ((base[c] + own_use * full_in[c].astype(F32)) / N).astype(BF16)
            return carry

        def values_copies():
            return [wide_copy(d, values_in.at[wide], values_in.at[wide], vws, vwr) for d in range(1, W)]

        LAG, HEAD, PER = 2, groups // 2, groups // 4
        lax.fori_loop(0, latents // LANES, flip, 0)
        lax.fori_loop(0, HEAD, more_slots, 0)
        for c in range(plain):
            send_msg(c, 0)
            if c >= LAG:
                send_err(c - LAG, 0)
            if c == 0:
                pair_values().wait_recv()
                for copy in values_copies():
                    copy.start()
            if c < 2:
                lax.fori_loop(HEAD + c * PER, HEAD + (c + 1) * PER, more_slots, 0)
            if c == 2:
                for copy in values_copies():
                    copy.wait_recv()
                fill(values_in, slot_in, lat_in)
        for i in range(early * PARTS):
            dec_copy(i).wait_recv()
        lax.fori_loop(0, early, send_full, 0)
        for c in range(plain - LAG, plain):
            send_err(c, 0)

        def arrive(c):
            err_copy(c).wait_recv()

        def finish(c, carry):
            rec_copy(c).wait_send()
            msg_copy(c).wait_send()
            err_copy(c).wait_send()
            return carry

        def finish_early():
            for i in range(early * PARTS):
                dec_copy(i).wait_send()
            for c in range(early):
                full_copy(c).wait_send()
            pair_values().wait_send()
            for copy in values_copies():
                copy.wait_send()
    else:
        plain = chunks

        def goal_of(d):
            return lax.rem(narrow + d, N)

        def rec_copy(c, d):
            return narrow_copy(goal_of(d), rec.at[c, goal_of(d)], rec_in.at[c, d], ns1.at[c, d], nr1.at[c, d])

        def err_copy(c, d):
            return narrow_copy(
                goal_of(d), err_out.at[c, d], err.at[own_rows(narrow), columns(c)], ns2.at[c, d], nr2.at[c, d]
            )

        def send_rec(c, carry):
            rec[c] = decode(c).astype(BF16).reshape(N, own, chunk)
            for d in range(1, N):
                rec_copy(c, d).start()
            return carry

        lax.fori_loop(0, chunks, send_rec, 0)

        def combine(c, carry):
            for d in range(1, N):
                rec_copy(c, d).wait_recv()
            shift = shift_ref[:, columns(c)] - act[own_rows(narrow), columns(c)].astype(F32)
            terms = [rec[c, narrow].astype(F32)]
            terms += [rec_in[c, d].astype(F32) for d in range(1, N)]
            for e in range(N):
                goal = goal_of(e)
                back = (N - goal).astype(F32) * shift
                for d in range(N):
                    origin = lax.rem(narrow + N - d, N)
                    back = back + (N - jnp.maximum(goal, origin)).astype(F32) * terms[d]
                back = (back / N).astype(BF16)
                if e == 0:
                    err[own_rows(narrow), columns(c)] = back
                else:
                    err_out[c, e] = back
                    err_copy(c, e).start()
            return carry

        lax.fori_loop(0, chunks, combine, 0)
        lax.fori_loop(0, latents // LANES, flip, 0)

        def arrive(c):
            for d in range(1, N):
                err_copy(c, d).wait_recv()

        def finish(c, carry):
            for d in range(1, N):
                rec_copy(c, d).wait_send()
                err_copy(c, d).wait_send()
            return carry

        def finish_early():
            pass

    def contract(c):
        return lax.dot_general(
            err[:, columns(c)], dec[:, columns(c)], (((1,), (1,)), ((), ())), preferred_element_type=F32
        )

    def outer(c):
        dg_ref[:, columns(c)] = jnp.dot(lat_t[...], err[:, columns(c)], preferred_element_type=F32).astype(BF16)

    total[...] = jnp.zeros_like(total)

    def local_chunk(c, carry):
        total[...] += contract(c)
        outer(c)
        return carry

    def sent_chunk(c, carry):
        arrive(c)
        return local_chunk(c, carry)

    if early:
        lax.fori_loop(0, plain // 2, sent_chunk, 0)
        lax.fori_loop(0, early, take_full, 0)
        lax.fori_loop(plain, chunks, local_chunk, 0)
        lax.fori_loop(plain // 2, plain - 1, sent_chunk, 0)
    else:
        lax.fori_loop(0, plain - 1, sent_chunk, 0)
    arrive(plain - 1)
    total[...] += contract(plain - 1)

    def pack(w, carry):
        picked = pick_dense(w)
        mine[w] = picked
        lg_packed[w] = picked.astype(BF16)
        return carry

    for w in range(W):
        pack(w, 0)
    for d in range(1, W):
        scatter_copy(d, lg_packed, grad_in, ws3, wr3).start()
    outer(plain - 1)
    summed = mine[wide]
    for d in range(1, W):
        scatter_copy(d, lg_packed, grad_in, ws3, wr3).wait_recv()
        summed = summed + grad_in[d].astype(F32)
    for p in range(fold):
        grad_ref[p * rows : (p + 1) * rows, :] = spread(summed, slot, wide, p)

    for d in range(1, W):
        scatter_copy(d, part, wide_in, ws1, wr1).wait_send()
        wide_copy(d, values.at[wide], values.at[wide], ws2, wr2).wait_send()
        scatter_copy(d, lg_packed, grad_in, ws3, wr3).wait_send()

    lax.fori_loop(0, plain, finish, 0)
    finish_early()


STORES = 4


def store_kernel(dg_ref, grad_ref, dg_hbm, grad_hbm, sem):
    step = dg_ref.shape[0] // STORES
    copies = [pltpu.make_async_copy(grad_ref, grad_hbm, sem.at[STORES])]
    for i in range(STORES):
        at = pl.ds(i * step, step)
        copies.append(pltpu.make_async_copy(dg_ref.at[at], dg_hbm.at[at], sem.at[i]))
    for copy in copies:
        copy.start()
    for copy in copies:
        copy.wait()


def local(activations, enc_weight, enc_bias, dec_weight, dec_bias, active_ids):
    W, N = lax.axis_size("wide"), lax.axis_size("narrow")
    tokens, channels = activations.shape
    latents = enc_weight.shape[1]
    top = active_ids.shape[1]
    fold = LANES // top
    rows = tokens // W // fold
    chunk = min(channels, 256)
    chunks = channels // chunk
    pieces = 4
    own = tokens // N
    early = chunks // 8 if N == 4 else 0
    plain = chunks - early
    half = (plain, tokens // 2, chunk)
    packed_shape = (W, rows, LANES)
    vmem = pl.BlockSpec(memory_space=pltpu.VMEM)
    hbm = pl.BlockSpec(memory_space=pl.ANY)
    dma = pltpu.SemaphoreType.DMA
    if early:
        scratch = [
            pltpu.VMEM((latents, early * chunk), BF16),
            pltpu.VMEM((tokens, latents), jnp.int16),
            pltpu.VMEM(packed_shape, BF16),
            pltpu.VMEM((tokens, latents), BF16),
            pltpu.VMEM((plain, 2, tokens // 2, chunk), BF16),
            *[pltpu.VMEM(half, BF16)] * 4,
            *[pltpu.VMEM((early, tokens, chunk), BF16)] * 2,
            pltpu.VMEM((early, tokens, chunk), F32),
            dma((2 * early,)), dma((2 * early,)), dma((1,)), dma((1,)), dma((W,)), dma((W,)),
            *[dma((plain,))] * 6,
            dma((early,)), dma((early,)),
        ]
    else:
        scratch = [*[pltpu.VMEM((chunks, N, own, chunk), BF16)] * 3, *[dma((chunks, N))] * 4]
    dec_grad, latent_grad = pl.pallas_call(
        functools.partial(step_kernel, W, N, fold, top, chunk, pieces, early),
        out_shape=(
            pltpu.VMEM((latents, channels), BF16),
            pltpu.VMEM((tokens // W, latents), F32),
        ),
        in_specs=[vmem, vmem, vmem, hbm, hbm, hbm],
        out_specs=(vmem, vmem),
        scratch_shapes=[
            pltpu.VMEM((tokens, LANES), jnp.int32),
            pltpu.VMEM((tokens, channels), BF16),
            pltpu.VMEM((channels, latents), BF16),
            pltpu.VMEM((latents, channels), BF16),
            pltpu.VMEM((tokens, latents), jnp.int16),
            pltpu.VMEM((tokens, latents), F32),
            pltpu.VMEM(packed_shape, F32),
            pltpu.VMEM(packed_shape, BF16),
            pltpu.VMEM(packed_shape, BF16),
            pltpu.VMEM(packed_shape, BF16),
            pltpu.VMEM((tokens, latents), BF16),
            pltpu.VMEM((latents, tokens), BF16),
            pltpu.VMEM((tokens, channels), BF16),
            pltpu.VMEM(packed_shape, BF16),
            pltpu.VMEM(packed_shape, BF16),
            dma((3 + pieces,)),
            *[dma((W,))] * 6,
            *scratch,
        ],
        compiler_params=pltpu.CompilerParams(collective_id=0, has_side_effects=True, vmem_limit_bytes=56 * 2**20),
        cost_estimate=pl.CostEstimate(
            flops=8 * tokens * channels * latents, bytes_accessed=6 * channels * (tokens + latents), transcendentals=0
        ),
        name="step",
    )(active_ids.T, enc_bias.reshape(1, -1), dec_bias.reshape(1, -1), activations, enc_weight, dec_weight)
    return pl.pallas_call(
        store_kernel,
        out_shape=(
            jax.ShapeDtypeStruct(dec_grad.shape, BF16),
            jax.ShapeDtypeStruct(latent_grad.shape, F32),
        ),
        in_specs=[vmem, vmem],
        out_specs=(hbm, hbm),
        scratch_shapes=[dma((STORES + 1,))],
        compiler_params=pltpu.CompilerParams(vmem_limit_bytes=2**20),
        name="store",
    )(
        pltpu.with_memory_space_constraint(dec_grad, pltpu.VMEM),
        pltpu.with_memory_space_constraint(latent_grad, pltpu.VMEM),
    )


def solution(mesh):
    in_specs = (
        P(None, "wide"),
        P("wide", "narrow"),
        P("narrow"),
        P("narrow", "wide"),
        P("wide"),
        P(),
    )
    out_specs = (P("narrow", "wide"), P("wide", "narrow"))
    return jax.shard_map(local, mesh=mesh, in_specs=in_specs, out_specs=out_specs, check_vma=False)
```

time: 80.7 us -> 71.7 us (0.89)
  Pallas kernels: 77.2 us -> 70.9 us
  local copies, waits for them, and re-layouts: 2.72 us -> 0 us
    pallas_call x1, Pallas kernels: 77.2 us -> 68.8 us  [local(): pl.pallas_call(functools.partial(step_kernel, W, N, fold, top, chunk, pie...]
    unnamed x2 -> x0, local copies, waits for them, and re-layouts: 2.72 us -> none
    pallas_call x0 -> x1, Pallas kernels: none -> 2.14 us  [local(): pl.pallas_call(store_kernel, out_shape=(jax.ShapeDtypeStruct(dec_grad.sha...]
where the time goes in v2:
time: 71.7 us; the launch traced here: 71.6 us
  Pallas kernels  70.9 us (99%)
    pallas_call x1, Pallas kernels, local(): pl.pallas_call(functools.partial(step_kernel, W, N, fold, top, chunk, pie...  68.8 us
    pallas_call x1, Pallas kernels, local(): pl.pallas_call(store_kernel, out_shape=(jax.ShapeDtypeStruct(dec_grad.sha...  2.14 us

profile of v2, /device:TPU:0, one launch (start us, length us, event | category | flops | bytes accessed | tf_op | source)
XLA Modules:
  0.0 71.6 jit_solution(12583355634151871870)
XLA Ops:
  0.6 68.8 %step.1 = (bf16[1024,2048]{1,0:T(8,128)(2,1)S(1)}, f32[64,1024]{1,0:T(8,128)S(1)}) custom-call(s32[64,512]{1,0:T(8,128)} %bitcast.3, f32[1,1024]{1,0:T(1,128)} %bitcast.5, f32[1,2048]{1,0:T(1,128)} %bitcast.4, bf16[512,2048]{1,0:T(8,128)(2,1)} %act_hbm.1, bf16[2048,1024]{1,0:T(8,128)(2,1)} %enc_hbm.1, bf16[1024,2048]{1,0:T(8,128)(2,1)} %dec_hbm.1), custom_call_target="tpu_custom_call" | custom-call | flops 8589934592 | bytes 18874368 | tf_op jit(solution)/shard_map/step/pallas_call | solution.py:502
  69.4 2.1 %store.1 = (bf16[1024,2048]{1,0:T(8,128)(2,1)}, f32[64,1024]{1,0:T(8,128)}) custom-call(bf16[1024,2048]{1,0:T(8,128)(2,1)S(1)} %get-tuple-element.4.dg_ref, f32[64,1024]{1,0:T(8,128)S(1)} %get-tuple-element.5.grad_ref), custom_call_target="tpu_custom_call" | custom-call | tf_op jit(solution)/shard_map/store/pallas_call | solution.py:536

commit v3 on v2

--- a/solution.py
+++ b/solution.py
@@ -27,11 +27,17 @@
     return picked
 
 
+def spread_row(table, p, top, tiles, slots):
+    rows = table.shape[0]
+    table = jnp.concatenate([table[:, p * top : (p + 1) * top], jnp.zeros((rows, LANES - top), F32)], axis=1)
+    return jnp.concatenate([lookup(table, slots(j)) for j in range(tiles)], axis=1)
+
+
 def step_kernel(
     W, N, fold, top, chunk, pieces, early,
     ids_t_ref, bias_ref, shift_ref, act_hbm, enc_hbm, dec_hbm,
-    dg_ref, grad_ref,
-    ids, act, enc, dec, slot, total, mine, part, wide_in, values, lat, lat_t,
+    dg_ref, sum_ref, own_slot_ref,
+    ids, act, enc, dec, slot, total, part, wide_in, values, lat, lat_t,
     err, lg_packed, grad_in,
     load_sem, ws1, wr1, ws2, wr2, ws3, wr3, *scratch,
 ):
@@ -42,6 +48,18 @@
     chunks = channels // chunk
     piece = latents // pieces
     low = narrow * latents
+    half_rows, quarter = tokens // 2, tokens // 4
+    near = wide // (W // 2)
+
+    def mate(d):
+        goal = 0
+        for b in range(W.bit_length() - 1):
+            digit = wide // 2**b % 2
+            goal = goal + 2**b * (1 - digit if d >> b & 1 else digit)
+        return goal
+
+    def rows_of(h):
+        return pl.ds(pl.multiple_of(h * half_rows, half_rows), half_rows)
 
     def piece_cols(n):
         return pl.ds(pl.multiple_of(n * piece, LANES), piece)
@@ -63,7 +81,7 @@
 
     barrier = pltpu.get_barrier_semaphore()
     for d in range(1, W):
-        pl.semaphore_signal(barrier, inc=1, device_id={"wide": lax.rem(wide + d, W)}, device_id_type=MESH)
+        pl.semaphore_signal(barrier, inc=1, device_id={"wide": mate(d)}, device_id_type=MESH)
     for d in range(1, N):
         pl.semaphore_signal(barrier, inc=1, device_id={"narrow": lax.rem(narrow + d, N)}, device_id_type=MESH)
 
@@ -84,7 +102,7 @@
         for k in range(top):
             here = jnp.broadcast_to(ids_t_ref[k : k + 1, at] - offset, (GROUP, LANES)).astype(jnp.int16)
             found = [jnp.where(here == p, jnp.int16(k), f) for p, f in zip(places, found)]
-        slot[at, pl.ds(pl.multiple_of(band * TALL, TALL), TALL)] = jnp.concatenate(found, axis=0).T
+        slot[at, pl.ds(pl.multiple_of(band * TALL, TALL), TALL)] = jnp.concatenate(found, axis=0).T.astype(jnp.int32)
 
     def slots_of(i, carry):
         fill_slots(i, slot, low)
@@ -102,7 +120,7 @@
     def wide_copy(d, source, target, send, recv):
         return pltpu.make_async_remote_copy(
             src_ref=source, dst_ref=target, send_sem=send.at[d], recv_sem=recv.at[d],
-            device_id={"wide": lax.rem(wide + d, W)}, device_id_type=MESH,
+            device_id={"wide": mate(d)}, device_id_type=MESH,
         )
 
     def columns(c):
@@ -127,109 +145,121 @@
             )
 
         load_rest.wait()
-        for i in range(early * PARTS - 1):
+        for i in range(early * PARTS):
             dec_copy(i).start()
     else:
         rec, rec_in, err_out, ns1, nr1, ns2, nr2 = scratch
 
     load_act.wait()
 
-    def encode(n, carry):
-        pltpu.make_async_copy(enc_hbm.at[:, piece_cols(n)], enc.at[:, piece_cols(n)], load_sem.at[2 + n]).wait()
-        total[:, piece_cols(n)] = jnp.dot(act[...], enc[:, piece_cols(n)], preferred_element_type=F32)
+    def encode(h, n):
+        total[rows_of(h), piece_cols(n)] = jnp.dot(
+            act[rows_of(h), :], enc[:, piece_cols(n)], preferred_element_type=F32
+        )
+
+    def encode_far(n, carry):
+        load_enc(n).wait()
+        encode(1 - near, n)
         return carry
 
-    lax.fori_loop(0, pieces, encode, 0)
+    def encode_near(n, carry):
+        encode(near, n)
+        return carry
 
     half = lax.broadcasted_iota(jnp.int32, (rows, LANES), 1) // top
 
+    def block_rows(w, p):
+        return pl.ds(pl.multiple_of((w * fold + p) * rows, rows), rows)
+
     def packed_ids(w):
-        out = ids[pl.ds(w * (rows * fold), rows), :]
+        out = ids[block_rows(w, 0), :]
         for p in range(1, fold):
-            other = ids[pl.ds((w * fold + p) * rows, rows), :]
-            out = jnp.where(half == p, other, out)
+            out = jnp.where(half == p, ids[block_rows(w, p), :], out)
         return out - low
 
     def pick_dense(w):
         def tables(p):
-            at = pl.ds((w * fold + p) * rows, rows)
-            return [total[at, j * LANES : (j + 1) * LANES] for j in range(latents // LANES)]
+            return [total[block_rows(w, p), j * LANES : (j + 1) * LANES] for j in range(latents // LANES)]
 
         return pick(tables, packed_ids(w), fold, top)
 
-    def pick_block(w, carry):
-        picked = pick_dense(w)
-        mine[w] = picked
-        part[w] = picked.astype(BF16)
-        return carry
-
-    for w in range(W):
-        pick_block(w, 0)
-
     def scatter_copy(d, source, target, send, recv):
-        return wide_copy(d, source.at[lax.rem(wide + d, W)], target.at[d], send, recv)
-
-    for d in range(1, W):
-        scatter_copy(d, part, wide_in, ws1, wr1).start()
+        return wide_copy(d, source.at[d], target.at[d], send, recv)
+
+    def scatter(first, last, source, target, send, recv):
+        picked = None
+        for d in range(last - 1, first - 1, -1):
+            picked = pick_dense(mate(d))
+            if d > 0:
+                source[d] = picked.astype(BF16)
+                scatter_copy(d, source, target, send, recv).start()
+        return picked
+
+    def gather(picked, source, target, send, recv):
+        for d in range(1, W):
+            scatter_copy(d, source, target, send, recv).wait_recv()
+            picked = picked + target[d].astype(F32)
+        return picked
+
+    lax.fori_loop(0, pieces, encode_far, 0)
+    scatter(W // 2, W, part, wide_in, ws1, wr1)
+    lax.fori_loop(0, pieces, encode_near, 0)
+    summed = scatter(0, W // 2, part, wide_in, ws1, wr1)
 
     def bias_tables(p):
         return [jnp.broadcast_to(bias_ref[:, j * LANES : (j + 1) * LANES], (rows, LANES)) for j in range(latents // LANES)]
 
-    summed = mine[wide] + pick(bias_tables, packed_ids(wide), fold, top)
-
-    lax.fori_loop(groups // 4, groups * 5 // 8, slots_of, 0)
-
-    for d in range(1, W):
-        scatter_copy(d, part, wide_in, ws1, wr1).wait_recv()
-        summed = summed + wide_in[d].astype(F32)
-    values[wide] = summed.astype(BF16)
-    for d in range(1, W):
-        wide_copy(d, values.at[wide], values.at[wide], ws2, wr2).start()
+    summed = summed + pick(bias_tables, packed_ids(wide), fold, top)
+
+    lax.fori_loop(groups // 4, groups * 3 // 4, slots_of, 0)
+
+    values[wide] = gather(summed, part, wide_in, ws1, wr1).astype(BF16)
+
+    def value_copy(d):
+        return wide_copy(d, values.at[wide], values.at[wide], ws2, wr2)
+
+    for d in range(W - 1, 0, -1):
+        value_copy(d).start()
     if early:
         def pair_values():
             return narrow_copy(across, values.at[wide], values_in.at[wide], vs.at[0], vr.at[0])
 
         pair_values().start()
-        dec_copy(early * PARTS - 1).start()
-
-    lax.fori_loop(groups * 5 // 8, groups, slots_of, 0)
-    for d in range(1, W):
-        wide_copy(d, values.at[wide], values.at[wide], ws2, wr2).wait_recv()
-
-    def spread(table, slot, block, p):
-        start = (block * fold + p) * rows
-        at = pl.ds(start if isinstance(start, int) else pl.multiple_of(start, rows), rows)
-        table = table[:, p * top : (p + 1) * top]
-        table = jnp.concatenate([table, jnp.zeros((rows, LANES - top), F32)], axis=1)
-        out = []
-        for j in range(latents // LANES):
-            out.append(lookup(table, slot[at, j * LANES : (j + 1) * LANES].astype(jnp.int32)))
-        return jnp.concatenate(out, axis=1)
-
-    def fill(values, slot, lat):
-        for block in range(W):
-            table = values[block].astype(F32)
-            both = jnp.concatenate([spread(table, slot, block, p) for p in range(fold)], axis=0)
-            lat[block * (fold * rows) : (block + 1) * (fold * rows), :] = both.astype(BF16)
-
-    fill(values, slot, lat)
+
+    lax.fori_loop(groups * 3 // 4, groups, slots_of, 0)
+
+    def fill_block(block, values, slot, lat):
+        table = values[block].astype(F32)
+        for p in range(fold):
+            at = block_rows(block, p)
+            spread = spread_row(table, p, top, latents // LANES, lambda j: slot[at, j * LANES : (j + 1) * LANES])
+            lat[at, :] = spread.astype(BF16)
+
+    def fill_mates(first, last):
+        for d in range(first, last):
+            if d > 0:
+                value_copy(d).wait_recv()
+            fill_block(mate(d), values, slot, lat)
+
     load_dec.wait()
 
     def own_rows(i):
         return pl.ds(pl.multiple_of(i * own, own), own)
+
+    def keep_slots():
+        own_slot_ref[...] = slot[pl.ds(pl.multiple_of(wide * (fold * rows), fold * rows), fold * rows), :]
 
     def flip(j, carry):
         at = pl.ds(pl.multiple_of(j * LANES, LANES), LANES)
         lat_t[at, :] = lat[:, at].T
         return carry
 
-    def decode(c):
-        return jnp.dot(lat[...], dec[:, columns(c)], preferred_element_type=F32)
+    def decode(c, at=slice(None)):
+        return jnp.dot(lat[at, :], dec[:, columns(c)], preferred_element_type=F32)
 
     if early:
-        mates = N // 2
-        share = tokens // mates
-        here = pl.ds(pl.multiple_of(side * share, share), share)
+        def here(h):
+            return pl.ds(pl.multiple_of(h * half_rows + side * quarter, quarter), quarter)
 
         def scale(count):
             return count.astype(F32)
@@ -238,46 +268,55 @@
         least = scale(N - jnp.maximum(narrow, across))
         own_use, mate_use = scale(1 + pair * (N - 1 - narrow)), scale(1 + pair * (N - 1 - across))
 
-        def rec_copy(c):
-            return narrow_copy(across, rec.at[c, 1 - side], rec_in.at[c], ns1.at[c], nr1.at[c])
+        def rec_copy(c, q):
+            h = near if q == 0 else 1 - near
+            return narrow_copy(across, rec.at[c, h, 1 - side], rec_in.at[c, h], ns1.at[c, q], nr1.at[c, q])
 
         def msg_copy(c):
             return narrow_copy(along, msg.at[c], msg_in.at[c], ns2.at[c], nr2.at[c])
 
-        def err_copy(c):
-            return narrow_copy(across, err_out.at[c], err.at[here, columns(c)], ns3.at[c], nr3.at[c])
+        def err_copy(c, h):
+            return narrow_copy(across, err_out.at[c, h], err.at[here(h), columns(c)], ns3.at[c, h], nr3.at[c, h])
 
         def full_copy(c):
             return narrow_copy(along, full.at[c], full_in.at[c], fs.at[c], fr.at[c])
 
-        def send_rec(c, carry):
-            rec[c] = decode(c).astype(BF16).reshape(mates, share, chunk)
-            rec_copy(c).start()
-            return carry
-
-        lax.fori_loop(0, plain, send_rec, 0)
+        def send_rec(q):
+            h = near if q == 0 else 1 - near
+
+            def send(c, carry):
+                rec[c, h] = decode(c, rows_of(h)).astype(BF16).reshape(2, quarter, chunk)
+                rec_copy(c, q).start()
+                return carry
+
+            lax.fori_loop(0, plain, send, 0)
+
+        fill_mates(0, W // 2)
+        send_rec(0)
+        fill_mates(W // 2, W)
+        send_rec(1)
 
         def more_slots(i, carry):
             fill_slots(i, slot_in, across * latents)
             return carry
 
-        def send_msg(c, carry):
-            rec_copy(c).wait_recv()
-            msg[c] = (own_use * rec[c, side].astype(F32) + mate_use * rec_in[c].astype(F32)).astype(BF16)
+        def send_msg(c):
+            for q in range(2):
+                rec_copy(c, q).wait_recv()
+            msg[c] = (own_use * rec[c, :, side].astype(F32) + mate_use * rec_in[c].astype(F32)).astype(BF16)
             msg_copy(c).start()
-            return carry
-
-        def send_err(c, carry):
+
+        def send_err(c):
             msg_copy(c).wait_recv()
-            shift = shift_ref[:, columns(c)] - act[here, columns(c)].astype(F32)
-            mine_rec, mate_rec = rec[c, side].astype(F32), rec_in[c].astype(F32)
-            other = msg_in[c].astype(F32)
-            back = own_scale * (shift + mine_rec) + least * mate_rec + own_use * other
-            err[here, columns(c)] = (back / N).astype(BF16)
-            back = mate_scale * (shift + mate_rec) + least * mine_rec + mate_use * other
-            err_out[c] = (back / N).astype(BF16)
-            err_copy(c).start()
-            return carry
+            for h in range(2):
+                shift = shift_ref[:, columns(c)] - act[here(h), columns(c)].astype(F32)
+                mine_rec, mate_rec = rec[c, h, side].astype(F32), rec_in[c, h].astype(F32)
+                other = msg_in[c, h].astype(F32)
+                back = mate_scale * (shift + mate_rec) + least * mine_rec + mate_use * other
+                err_out[c, h] = (back / N).astype(BF16)
+                err_copy(c, h).start()
+                back = own_scale * (shift + mine_rec) + least * mate_rec + own_use * other
+                err[here(h), columns(c)] = (back / N).astype(BF16)
 
         def send_full(c, carry):
             mine_rec = decode(plain + c)
@@ -297,12 +336,13 @@
             return [wide_copy(d, values_in.at[wide], values_in.at[wide], vws, vwr) for d in range(1, W)]
 
         LAG, HEAD, PER = 2, groups // 2, groups // 4
+        keep_slots()
         lax.fori_loop(0, latents // LANES, flip, 0)
         lax.fori_loop(0, HEAD, more_slots, 0)
         for c in range(plain):
-            send_msg(c, 0)
+            send_msg(c)
             if c >= LAG:
-                send_err(c - LAG, 0)
+                send_err(c - LAG)
             if c == 0:
                 pair_values().wait_recv()
                 for copy in values_copies():
@@ -312,20 +352,23 @@
             if c == 2:
                 for copy in values_copies():
                     copy.wait_recv()
-                fill(values_in, slot_in, lat_in)
+                for block in range(W):
+                    fill_block(block, values_in, slot_in, lat_in)
         for i in range(early * PARTS):
             dec_copy(i).wait_recv()
         lax.fori_loop(0, early, send_full, 0)
         for c in range(plain - LAG, plain):
-            send_err(c, 0)
+            send_err(c)
 
         def arrive(c):
-            err_copy(c).wait_recv()
+            for h in range(2):
+                err_copy(c, h).wait_recv()
 
         def finish(c, carry):
-            rec_copy(c).wait_send()
+            for q in range(2):
+                rec_copy(c, q).wait_send()
+                err_copy(c, q).wait_send()
             msg_copy(c).wait_send()
-            err_copy(c).wait_send()
             return carry
 
         def finish_early():
@@ -338,6 +381,8 @@
                 copy.wait_send()
     else:
         plain = chunks
+        fill_mates(0, W)
+        keep_slots()
 
         def goal_of(d):
             return lax.rem(narrow + d, N)
@@ -423,27 +468,13 @@
     arrive(plain - 1)
     total[...] += contract(plain - 1)
 
-    def pack(w, carry):
-        picked = pick_dense(w)
-        mine[w] = picked
-        lg_packed[w] = picked.astype(BF16)
-        return carry
-
-    for w in range(W):
-        pack(w, 0)
-    for d in range(1, W):
-        scatter_copy(d, lg_packed, grad_in, ws3, wr3).start()
+    summed = scatter(0, W, lg_packed, grad_in, ws3, wr3)
     outer(plain - 1)
-    summed = mine[wide]
-    for d in range(1, W):
-        scatter_copy(d, lg_packed, grad_in, ws3, wr3).wait_recv()
-        summed = summed + grad_in[d].astype(F32)
-    for p in range(fold):
-        grad_ref[p * rows : (p + 1) * rows, :] = spread(summed, slot, wide, p)
+    sum_ref[...] = gather(summed, lg_packed, grad_in, ws3, wr3)
 
     for d in range(1, W):
         scatter_copy(d, part, wide_in, ws1, wr1).wait_send()
-        wide_copy(d, values.at[wide], values.at[wide], ws2, wr2).wait_send()
+        value_copy(d).wait_send()
         scatter_copy(d, lg_packed, grad_in, ws3, wr3).wait_send()
 
     lax.fori_loop(0, plain, finish, 0)
@@ -453,14 +484,18 @@
 STORES = 4
 
 
-def store_kernel(dg_ref, grad_ref, dg_hbm, grad_hbm, sem):
+def store_kernel(fold, top, dg_ref, sum_ref, slot_ref, dg_hbm, grad_ref, sem):
     step = dg_ref.shape[0] // STORES
-    copies = [pltpu.make_async_copy(grad_ref, grad_hbm, sem.at[STORES])]
+    rows = sum_ref.shape[0]
+    copies = []
     for i in range(STORES):
         at = pl.ds(i * step, step)
         copies.append(pltpu.make_async_copy(dg_ref.at[at], dg_hbm.at[at], sem.at[i]))
     for copy in copies:
         copy.start()
+    for p in range(fold):
+        at = slice(p * rows, (p + 1) * rows)
+        grad_ref[at, :] = spread_row(sum_ref[...], p, top, slot_ref.shape[1] // LANES, lambda j: slot_ref[at, j * LANES : (j + 1) * LANES])
     for copy in copies:
         copy.wait()
 
@@ -478,7 +513,7 @@
     own = tokens // N
     early = chunks // 8 if N == 4 else 0
     plain = chunks - early
-    half = (plain, tokens // 2, chunk)
+    half = (plain, 2, tokens // 4, chunk)
     packed_shape = (W, rows, LANES)
     vmem = pl.BlockSpec(memory_space=pltpu.VMEM)
     hbm = pl.BlockSpec(memory_space=pl.ANY)
@@ -486,35 +521,35 @@
     if early:
         scratch = [
             pltpu.VMEM((latents, early * chunk), BF16),
-            pltpu.VMEM((tokens, latents), jnp.int16),
+            pltpu.VMEM((tokens, latents), jnp.int32),
             pltpu.VMEM(packed_shape, BF16),
             pltpu.VMEM((tokens, latents), BF16),
-            pltpu.VMEM((plain, 2, tokens // 2, chunk), BF16),
+            pltpu.VMEM((plain, 2, 2, tokens // 4, chunk), BF16),
             *[pltpu.VMEM(half, BF16)] * 4,
             *[pltpu.VMEM((early, tokens, chunk), BF16)] * 2,
             pltpu.VMEM((early, tokens, chunk), F32),
             dma((2 * early,)), dma((2 * early,)), dma((1,)), dma((1,)), dma((W,)), dma((W,)),
-            *[dma((plain,))] * 6,
+            *[dma((plain, 2))] * 2, *[dma((plain,))] * 2, *[dma((plain, 2))] * 2,
             dma((early,)), dma((early,)),
         ]
     else:
         scratch = [*[pltpu.VMEM((chunks, N, own, chunk), BF16)] * 3, *[dma((chunks, N))] * 4]
-    dec_grad, latent_grad = pl.pallas_call(
+    dec_grad, summed, slots = pl.pallas_call(
         functools.partial(step_kernel, W, N, fold, top, chunk, pieces, early),
         out_shape=(
             pltpu.VMEM((latents, channels), BF16),
-            pltpu.VMEM((tokens // W, latents), F32),
+            pltpu.VMEM((rows, LANES), F32),
+            pltpu.VMEM((tokens // W, latents), jnp.int32),
         ),
         in_specs=[vmem, vmem, vmem, hbm, hbm, hbm],
-        out_specs=(vmem, vmem),
+        out_specs=(vmem, vmem, vmem),
         scratch_shapes=[
             pltpu.VMEM((tokens, LANES), jnp.int32),
             pltpu.VMEM((tokens, channels), BF16),
             pltpu.VMEM((channels, latents), BF16),
             pltpu.VMEM((latents, channels), BF16),
-            pltpu.VMEM((tokens, latents), jnp.int16),
+            pltpu.VMEM((tokens, latents), jnp.int32),
             pltpu.VMEM((tokens, latents), F32),
-            pltpu.VMEM(packed_shape, F32),
             pltpu.VMEM(packed_shape, BF16),
             pltpu.VMEM(packed_shape, BF16),
             pltpu.VMEM(packed_shape, BF16),
@@ -533,21 +568,19 @@
         ),
         name="step",
     )(active_ids.T, enc_bias.reshape(1, -1), dec_bias.reshape(1, -1), activations, enc_weight, dec_weight)
+    resident = [pltpu.with_memory_space_constraint(x, pltpu.VMEM) for x in (dec_grad, summed, slots)]
     return pl.pallas_call(
-        store_kernel,
+        functools.partial(store_kernel, fold, top),
         out_shape=(
-            jax.ShapeDtypeStruct(dec_grad.shape, BF16),
-            jax.ShapeDtypeStruct(latent_grad.shape, F32),
+            jax.ShapeDtypeStruct((latents, channels), BF16),
+            jax.ShapeDtypeStruct((tokens // W, latents), F32),
         ),
-        in_specs=[vmem, vmem],
-        out_specs=(hbm, hbm),
-        scratch_shapes=[dma((STORES + 1,))],
+        in_specs=[vmem, vmem, vmem],
+        out_specs=(hbm, vmem),
+        scratch_shapes=[dma((STORES,))],
         compiler_params=pltpu.CompilerParams(vmem_limit_bytes=2**20),
         name="store",
-    )(
-        pltpu.with_memory_space_constraint(dec_grad, pltpu.VMEM),
-        pltpu.with_memory_space_constraint(latent_grad, pltpu.VMEM),
-    )
+    )(*resident)
 
 
 def solution(mesh):

time: 71.7 us -> 70.9 us (0.989)
  Pallas kernels: 70.9 us -> 70.1 us
    pallas_call x1, Pallas kernels: 68.8 us -> 67.2 us  [local(): pl.pallas_call(functools.partial(step_kernel, W, N, fold, top, chunk, pie...]
    pallas_call x1, Pallas kernels: 2.14 us -> 2.91 us  [local(): pl.pallas_call(functools.partial(store_kernel, fold, top), out_shape=(jax...]
where the time goes in v3:
time: 70.9 us; the launch traced here: 70.8 us
  Pallas kernels  70.1 us (99%)
    pallas_call x1, Pallas kernels, local(): pl.pallas_call(functools.partial(step_kernel, W, N, fold, top, chunk, pie...  67.2 us
    pallas_call x1, Pallas kernels, local(): pl.pallas_call(functools.partial(store_kernel, fold, top), out_shape=(jax...  2.91 us

profile of v3, /device:TPU:0, one launch (start us, length us, event | category | flops | bytes accessed | tf_op | source)
XLA Modules:
  0.0 70.8 jit_solution(8671297403020242544)
XLA Ops:
  0.6 67.2 %step.1 = (bf16[1024,2048]{1,0:T(8,128)(2,1)S(1)}, f32[32,128]{1,0:T(8,128)S(1)}, s32[64,1024]{1,0:T(8,128)S(1)}) custom-call(s32[64,512]{1,0:T(8,128)} %bitcast.3, f32[1,1024]{1,0:T(1,128)} %bitcast.5, f32[1,2048]{1,0:T(1,128)} %bitcast.4, bf16[512,2048]{1,0:T(8,128)(2,1)} %act_hbm.1, bf16[2048,1024]{1,0:T(8,128)(2,1)} %enc_hbm.1, bf16[1024,2048]{1,0:T(8,128)(2,1)} %dec_hbm.1), custom_call_target="tpu_custom_call" | custom-call | flops 8589934592 | bytes 18874368 | tf_op jit(solution)/shard_map/step/pallas_call | solution.py:537
  67.9 2.9 %store.1 = (bf16[1024,2048]{1,0:T(8,128)(2,1)}, f32[64,1024]{1,0:T(8,128)}) custom-call(bf16[1024,2048]{1,0:T(8,128)(2,1)S(1)} %get-tuple-element.5.dg_ref, f32[32,128]{1,0:T(8,128)S(1)} %get-tuple-element.6.sum_ref, s32[64,1024]{1,0:T(8,128)S(1)} %get-tuple-element.7.slot_ref), custom_call_target="tpu_custom_call" | custom-call | tf_op jit(solution)/shard_map/store/pallas_call | solution.py:572

commit v4 on v3

--- a/solution.py
+++ b/solution.py
@@ -257,6 +257,19 @@
     def decode(c, at=slice(None)):
         return jnp.dot(lat[at, :], dec[:, columns(c)], preferred_element_type=F32)
 
+    def contract(c):
+        return lax.dot_general(
+            err[:, columns(c)], dec[:, columns(c)], (((1,), (1,)), ((), ())), preferred_element_type=F32
+        )
+
+    def outer(c):
+        dg_ref[:, columns(c)] = jnp.dot(lat_t[...], err[:, columns(c)], preferred_element_type=F32).astype(BF16)
+
+    def local_chunk(c, carry):
+        total[...] += contract(c)
+        outer(c)
+        return carry
+
     if early:
         def here(h):
             return pl.ds(pl.multiple_of(h * half_rows + side * quarter, quarter), quarter)
@@ -281,20 +294,24 @@
         def full_copy(c):
             return narrow_copy(along, full.at[c], full_in.at[c], fs.at[c], fr.at[c])
 
-        def send_rec(q):
+        def send_part(c, q):
             h = near if q == 0 else 1 - near
-
-            def send(c, carry):
-                rec[c, h] = decode(c, rows_of(h)).astype(BF16).reshape(2, quarter, chunk)
+            rec[c, h] = decode(c, rows_of(h)).astype(BF16).reshape(2, quarter, chunk)
+            rec_copy(c, q).start()
+
+        def send_rec(c, carry):
+            rec[c] = decode(c).astype(BF16).reshape(2, 2, quarter, chunk)
+            for q in range(2):
                 rec_copy(c, q).start()
-                return carry
-
-            lax.fori_loop(0, plain, send, 0)
+            return carry
 
         fill_mates(0, W // 2)
-        send_rec(0)
+        for c in range(FIRST):
+            send_part(c, 0)
         fill_mates(W // 2, W)
-        send_rec(1)
+        for c in range(FIRST):
+            send_part(c, 1)
+        lax.fori_loop(FIRST, plain, send_rec, 0)
 
         def more_slots(i, carry):
             fill_slots(i, slot_in, across * latents)
@@ -335,20 +352,27 @@
         def values_copies():
             return [wide_copy(d, values_in.at[wide], values_in.at[wide], vws, vwr) for d in range(1, W)]
 
-        LAG, HEAD, PER = 2, groups // 2, groups // 4
+        def arrive(c):
+            for h in range(2):
+                err_copy(c, h).wait_recv()
+
+        def take(c):
+            arrive(c)
+            local_chunk(c, 0)
+
+        pair_values().wait_recv()
+        for copy in values_copies():
+            copy.start()
         keep_slots()
         lax.fori_loop(0, latents // LANES, flip, 0)
-        lax.fori_loop(0, HEAD, more_slots, 0)
+        total[...] = jnp.zeros_like(total)
+        lax.fori_loop(0, groups // 2, more_slots, 0)
         for c in range(plain):
             send_msg(c)
             if c >= LAG:
                 send_err(c - LAG)
-            if c == 0:
-                pair_values().wait_recv()
-                for copy in values_copies():
-                    copy.start()
             if c < 2:
-                lax.fori_loop(HEAD + c * PER, HEAD + (c + 1) * PER, more_slots, 0)
+                lax.fori_loop((2 + c) * groups // 4, (3 + c) * groups // 4, more_slots, 0)
             if c == 2:
                 for copy in values_copies():
                     copy.wait_recv()
@@ -357,12 +381,10 @@
         for i in range(early * PARTS):
             dec_copy(i).wait_recv()
         lax.fori_loop(0, early, send_full, 0)
-        for c in range(plain - LAG, plain):
-            send_err(c)
-
-        def arrive(c):
-            for h in range(2):
-                err_copy(c, h).wait_recv()
+        for c in range(LAG):
+            send_err(plain - LAG + c)
+            take(c)
+
 
         def finish(c, carry):
             for q in range(2):
@@ -439,31 +461,16 @@
         def finish_early():
             pass
 
-    def contract(c):
-        return lax.dot_general(
-            err[:, columns(c)], dec[:, columns(c)], (((1,), (1,)), ((), ())), preferred_element_type=F32
-        )
-
-    def outer(c):
-        dg_ref[:, columns(c)] = jnp.dot(lat_t[...], err[:, columns(c)], preferred_element_type=F32).astype(BF16)
-
-    total[...] = jnp.zeros_like(total)
-
-    def local_chunk(c, carry):
-        total[...] += contract(c)
-        outer(c)
-        return carry
-
     def sent_chunk(c, carry):
         arrive(c)
         return local_chunk(c, carry)
 
     if early:
-        lax.fori_loop(0, plain // 2, sent_chunk, 0)
+        lax.fori_loop(LAG, plain - 1, sent_chunk, 0)
         lax.fori_loop(0, early, take_full, 0)
         lax.fori_loop(plain, chunks, local_chunk, 0)
-        lax.fori_loop(plain // 2, plain - 1, sent_chunk, 0)
     else:
+        total[...] = jnp.zeros_like(total)
         lax.fori_loop(0, plain - 1, sent_chunk, 0)
     arrive(plain - 1)
     total[...] += contract(plain - 1)
@@ -482,6 +489,7 @@
 
 
 STORES = 4
+FIRST, LAG = 3, 3
 
 
 def store_kernel(fold, top, dg_ref, sum_ref, slot_ref, dg_hbm, grad_ref, sem):

time: 70.9 us -> 69.2 us (0.976)
  Pallas kernels: 70.1 us -> 68.2 us
    pallas_call x1, Pallas kernels: 67.2 us -> 65.3 us  [local(): pl.pallas_call(functools.partial(step_kernel, W, N, fold, top, chunk, pie...]
where the time goes in v4:
time: 69.2 us; the launch traced here: 69 us
  Pallas kernels  68.2 us (99%)
  between operations  0.8 us (1%)
    pallas_call x1, Pallas kernels, local(): pl.pallas_call(functools.partial(step_kernel, W, N, fold, top, chunk, pie...  65.3 us
    pallas_call x1, Pallas kernels, local(): pl.pallas_call(functools.partial(store_kernel, fold, top), out_shape=(jax...  2.91 us

profile of v4, /device:TPU:0, one launch (start us, length us, event | category | flops | bytes accessed | tf_op | source)
XLA Modules:
  0.0 69.0 jit_solution(4370921847598242599)
XLA Ops:
  0.6 65.3 %step.1 = (bf16[1024,2048]{1,0:T(8,128)(2,1)S(1)}, f32[32,128]{1,0:T(8,128)S(1)}, s32[64,1024]{1,0:T(8,128)S(1)}) custom-call(s32[64,512]{1,0:T(8,128)} %bitcast.3, f32[1,1024]{1,0:T(1,128)} %bitcast.5, f32[1,2048]{1,0:T(1,128)} %bitcast.4, bf16[512,2048]{1,0:T(8,128)(2,1)} %act_hbm.1, bf16[2048,1024]{1,0:T(8,128)(2,1)} %enc_hbm.1, bf16[1024,2048]{1,0:T(8,128)(2,1)} %dec_hbm.1), custom_call_target="tpu_custom_call" | custom-call | flops 8589934592 | bytes 18874368 | tf_op jit(solution)/shard_map/step/pallas_call | solution.py:545
  66.0 2.9 %store.1 = (bf16[1024,2048]{1,0:T(8,128)(2,1)}, f32[64,1024]{1,0:T(8,128)}) custom-call(bf16[1024,2048]{1,0:T(8,128)(2,1)S(1)} %get-tuple-element.5.dg_ref, f32[32,128]{1,0:T(8,128)S(1)} %get-tuple-element.6.sum_ref, s32[64,1024]{1,0:T(8,128)S(1)} %get-tuple-element.7.slot_ref), custom_call_target="tpu_custom_call" | custom-call | tf_op jit(solution)/shard_map/store/pallas_call | solution.py:580

commit v5 on v4

--- a/solution.py
+++ b/solution.py
@@ -35,9 +35,9 @@
 
 def step_kernel(
     W, N, fold, top, chunk, pieces, early,
-    ids_t_ref, bias_ref, shift_ref, act_hbm, enc_hbm, dec_hbm,
+    ids_hbm, bias_hbm, shift_hbm, act_hbm, enc_hbm, dec_hbm,
     dg_ref, sum_ref, own_slot_ref,
-    ids, act, enc, dec, slot, total, part, wide_in, values, lat, lat_t,
+    ids_t_ref, bias_ref, shift_ref, ids, act, enc, dec, slot, total, part, wide_in, values, lat, lat_t,
     err, lg_packed, grad_in,
     load_sem, ws1, wr1, ws2, wr2, ws3, wr3, *scratch,
 ):
@@ -64,20 +64,27 @@
     def piece_cols(n):
         return pl.ds(pl.multiple_of(n * piece, LANES), piece)
 
-    load_act = pltpu.make_async_copy(act_hbm, act, load_sem.at[0])
-    head = channels - early * chunk
-    load_dec = pltpu.make_async_copy(dec_hbm.at[:, :head], dec.at[:, :head], load_sem.at[1])
+    def load(source, target, i):
+        return pltpu.make_async_copy(source, target, load_sem.at[i])
+
+    def load_act(h, i):
+        return load(act_hbm.at[rows_of(h)], act.at[rows_of(h)], i)
+
+    load_dec = load(dec_hbm, dec, 1)
+    load_ids = load(ids_hbm, ids_t_ref, 2)
+    load_bias = load(bias_hbm, bias_ref, 3)
+    load_shift = load(shift_hbm, shift_ref, 4)
 
     def load_enc(n):
-        return pltpu.make_async_copy(enc_hbm.at[:, piece_cols(n)], enc.at[:, piece_cols(n)], load_sem.at[2 + n])
-
-    if early:
-        load_rest = pltpu.make_async_copy(dec_hbm.at[:, head:], dec.at[:, head:], load_sem.at[2 + pieces])
-        load_rest.start()
-    load_act.start()
-    for n in range(pieces):
+        return load(enc_hbm.at[:, piece_cols(n)], enc.at[:, piece_cols(n)], 5 + n)
+
+    load_ids.start()
+    load_act(1 - near, 0).start()
+    for n in range(AHEAD):
         load_enc(n).start()
-    load_dec.start()
+    load_act(near, 5 + pieces).start()
+    load_bias.start()
+    load_shift.start()
 
     barrier = pltpu.get_barrier_semaphore()
     for d in range(1, W):
@@ -85,6 +92,9 @@
     for d in range(1, N):
         pl.semaphore_signal(barrier, inc=1, device_id={"narrow": lax.rem(narrow + d, N)}, device_id_type=MESH)
 
+    load_ids.wait()
+    for n in range(AHEAD, pieces):
+        load_enc(n).start()
     stacked = jnp.concatenate([ids_t_ref[...]] * fold, axis=0)
     ids[...] = stacked.T
 
@@ -108,7 +118,6 @@
         fill_slots(i, slot, low)
         return carry
 
-    lax.fori_loop(0, groups // 4, slots_of, 0)
     pl.semaphore_wait(barrier, W + N - 2)
 
     def narrow_copy(goal, source, target, send, recv):
@@ -141,16 +150,16 @@
         def dec_copy(i):
             c, at = i // PARTS, pl.ds(i % PARTS * tall, tall)
             return narrow_copy(
-                across, dec.at[at, columns(plain + c)], dec_in.at[at, columns(c)], ds.at[i], dr.at[i]
+                across, dec_hbm.at[at, columns(plain + c)], dec_in.at[at, columns(c)], ds.at[i], dr.at[i]
             )
 
-        load_rest.wait()
         for i in range(early * PARTS):
             dec_copy(i).start()
     else:
         rec, rec_in, err_out, ns1, nr1, ns2, nr2 = scratch
 
-    load_act.wait()
+    lax.fori_loop(0, groups // HEAD, slots_of, 0)
+    load_act(1 - near, 0).wait()
 
     def encode(h, n):
         total[rows_of(h), piece_cols(n)] = jnp.dot(
@@ -202,16 +211,20 @@
         return picked
 
     lax.fori_loop(0, pieces, encode_far, 0)
+    load_dec.start()
     scatter(W // 2, W, part, wide_in, ws1, wr1)
+    load_act(near, 5 + pieces).wait()
     lax.fori_loop(0, pieces, encode_near, 0)
     summed = scatter(0, W // 2, part, wide_in, ws1, wr1)
 
     def bias_tables(p):
         return [jnp.broadcast_to(bias_ref[:, j * LANES : (j + 1) * LANES], (rows, LANES)) for j in range(latents // LANES)]
 
+    load_bias.wait()
+    load_shift.wait()
     summed = summed + pick(bias_tables, packed_ids(wide), fold, top)
 
-    lax.fori_loop(groups // 4, groups * 3 // 4, slots_of, 0)
+    lax.fori_loop(groups // HEAD, groups * 3 // 4, slots_of, 0)
 
     values[wide] = gather(summed, part, wide_in, ws1, wr1).astype(BF16)
 
@@ -257,9 +270,9 @@
     def decode(c, at=slice(None)):
         return jnp.dot(lat[at, :], dec[:, columns(c)], preferred_element_type=F32)
 
-    def contract(c):
+    def contract(c, at=slice(None)):
         return lax.dot_general(
-            err[:, columns(c)], dec[:, columns(c)], (((1,), (1,)), ((), ())), preferred_element_type=F32
+            err[at, columns(c)], dec[:, columns(c)], (((1,), (1,)), ((), ())), preferred_element_type=F32
         )
 
     def outer(c):
@@ -473,9 +486,10 @@
         total[...] = jnp.zeros_like(total)
         lax.fori_loop(0, plain - 1, sent_chunk, 0)
     arrive(plain - 1)
-    total[...] += contract(plain - 1)
-
-    summed = scatter(0, W, lg_packed, grad_in, ws3, wr3)
+    total[rows_of(1 - near), :] += contract(plain - 1, rows_of(1 - near))
+    scatter(W // 2, W, lg_packed, grad_in, ws3, wr3)
+    total[rows_of(near), :] += contract(plain - 1, rows_of(near))
+    summed = scatter(0, W // 2, lg_packed, grad_in, ws3, wr3)
     outer(plain - 1)
     sum_ref[...] = gather(summed, lg_packed, grad_in, ws3, wr3)
 
@@ -489,10 +503,11 @@
 
 
 STORES = 4
+AHEAD, HEAD = 1, 8
 FIRST, LAG = 3, 3
 
 
-def store_kernel(fold, top, dg_ref, sum_ref, slot_ref, dg_hbm, grad_ref, sem):
+def store_kernel(fold, top, dg_ref, sum_ref, slot_ref, dg_hbm, grad_hbm, grad_ref, sem):
     step = dg_ref.shape[0] // STORES
     rows = sum_ref.shape[0]
     copies = []
@@ -504,6 +519,8 @@
     for p in range(fold):
         at = slice(p * rows, (p + 1) * rows)
         grad_ref[at, :] = spread_row(sum_ref[...], p, top, slot_ref.shape[1] // LANES, lambda j: slot_ref[at, j * LANES : (j + 1) * LANES])
+    copies.append(pltpu.make_async_copy(grad_ref, grad_hbm, sem.at[STORES]))
+    copies[-1].start()
     for copy in copies:
         copy.wait()
 
@@ -517,7 +534,7 @@
     rows = tokens // W // fold
     chunk = min(channels, 256)
     chunks = channels // chunk
-    pieces = 4
+    pieces = 1
     own = tokens // N
     early = chunks // 8 if N == 4 else 0
     plain = chunks - early
@@ -549,9 +566,12 @@
             pltpu.VMEM((rows, LANES), F32),
             pltpu.VMEM((tokens // W, latents), jnp.int32),
         ),
-        in_specs=[vmem, vmem, vmem, hbm, hbm, hbm],
+        in_specs=[hbm] * 6,
         out_specs=(vmem, vmem, vmem),
         scratch_shapes=[
+            pltpu.VMEM((top, tokens), jnp.int32),
+            pltpu.VMEM((1, latents), F32),
+            pltpu.VMEM((1, channels), F32),
             pltpu.VMEM((tokens, LANES), jnp.int32),
             pltpu.VMEM((tokens, channels), BF16),
             pltpu.VMEM((channels, latents), BF16),
@@ -566,7 +586,7 @@
             pltpu.VMEM((tokens, channels), BF16),
             pltpu.VMEM(packed_shape, BF16),
             pltpu.VMEM(packed_shape, BF16),
-            dma((3 + pieces,)),
+            dma((6 + pieces,)),
             *[dma((W,))] * 6,
             *scratch,
         ],
@@ -584,8 +604,8 @@
             jax.ShapeDtypeStruct((tokens // W, latents), F32),
         ),
         in_specs=[vmem, vmem, vmem],
-        out_specs=(hbm, vmem),
-        scratch_shapes=[dma((STORES,))],
+        out_specs=(hbm, hbm),
+        scratch_shapes=[pltpu.VMEM((tokens // W, latents), F32), dma((STORES + 1,))],
         compiler_params=pltpu.CompilerParams(vmem_limit_bytes=2**20),
         name="store",
     )(*resident)

time: 69.2 us -> 68.3 us (0.987)
  Pallas kernels: 68.2 us -> 67.4 us
where the time goes in v5:
time: 68.3 us; the launch traced here: 68.2 us
  Pallas kernels  67.4 us (99%)
  between operations  0.8 us (1%)
    pallas_call x1, Pallas kernels, local(): pl.pallas_call(functools.partial(step_kernel, W, N, fold, top, chunk, pie...  65.1 us
    pallas_call x1, Pallas kernels, local(): pl.pallas_call(functools.partial(store_kernel, fold, top), out_shape=(jax...  2.29 us

profile of v5, /device:TPU:0, one launch (start us, length us, event | category | flops | bytes accessed | tf_op | source)
XLA Modules:
  0.0 68.2 jit_solution(3182442526184357163)
XLA Ops:
  0.6 65.1 %step.1 = (bf16[1024,2048]{1,0:T(8,128)(2,1)S(1)}, f32[32,128]{1,0:T(8,128)S(1)}, s32[64,1024]{1,0:T(8,128)S(1)}) custom-call(s32[64,512]{1,0:T(8,128)} %bitcast.3, f32[1,1024]{1,0:T(1,128)} %bitcast.5, f32[1,2048]{1,0:T(1,128)} %bitcast.4, bf16[512,2048]{1,0:T(8,128)(2,1)} %act_hbm.1, bf16[2048,1024]{1,0:T(8,128)(2,1)} %enc_hbm.1, bf16[1024,2048]{1,0:T(8,128)(2,1)} %dec_hbm.1), custom_call_target="tpu_custom_call" | custom-call | flops 8589934592 | bytes 18874368 | tf_op jit(solution)/shard_map/step/pallas_call | solution.py:562
  65.7 2.3 %store.1 = (bf16[1024,2048]{1,0:T(8,128)(2,1)}, f32[64,1024]{1,0:T(8,128)}) custom-call(bf16[1024,2048]{1,0:T(8,128)(2,1)S(1)} %get-tuple-element.5.dg_ref, f32[32,128]{1,0:T(8,128)S(1)} %get-tuple-element.6.sum_ref, s32[64,1024]{1,0:T(8,128)S(1)} %get-tuple-element.7.slot_ref), custom_call_target="tpu_custom_call" | custom-call | tf_op jit(solution)/shard_map/store/pallas_call | solution.py:600

commit v6 on v5

--- a/solution.py
+++ b/solution.py
@@ -78,6 +78,12 @@
     def load_enc(n):
         return load(enc_hbm.at[:, piece_cols(n)], enc.at[:, piece_cols(n)], 5 + n)
 
+    barrier = pltpu.get_barrier_semaphore()
+    for d in range(1, W):
+        pl.semaphore_signal(barrier, inc=1, device_id={"wide": mate(d)}, device_id_type=MESH)
+    for d in range(1, N):
+        pl.semaphore_signal(barrier, inc=1, device_id={"narrow": lax.rem(narrow + d, N)}, device_id_type=MESH)
+
     load_ids.start()
     load_act(1 - near, 0).start()
     for n in range(AHEAD):
@@ -85,12 +91,6 @@
     load_act(near, 5 + pieces).start()
     load_bias.start()
     load_shift.start()
-
-    barrier = pltpu.get_barrier_semaphore()
-    for d in range(1, W):
-        pl.semaphore_signal(barrier, inc=1, device_id={"wide": mate(d)}, device_id_type=MESH)
-    for d in range(1, N):
-        pl.semaphore_signal(barrier, inc=1, device_id={"narrow": lax.rem(narrow + d, N)}, device_id_type=MESH)
 
     load_ids.wait()
     for n in range(AHEAD, pieces):
@@ -224,7 +224,7 @@
     load_shift.wait()
     summed = summed + pick(bias_tables, packed_ids(wide), fold, top)
 
-    lax.fori_loop(groups // HEAD, groups * 3 // 4, slots_of, 0)
+    lax.fori_loop(groups // HEAD, groups * TURN // 16, slots_of, 0)
 
     values[wide] = gather(summed, part, wide_in, ws1, wr1).astype(BF16)
 
@@ -239,7 +239,7 @@
 
         pair_values().start()
 
-    lax.fori_loop(groups * 3 // 4, groups, slots_of, 0)
+    lax.fori_loop(groups * TURN // 16, groups, slots_of, 0)
 
     def fill_block(block, values, slot, lat):
         table = values[block].astype(F32)
@@ -502,8 +502,8 @@
     finish_early()
 
 
-STORES = 4
-AHEAD, HEAD = 1, 8
+STORES = 1
+AHEAD, HEAD, TURN = 1, 8, 9
 FIRST, LAG = 3, 3
 
 

time: 68.3 us -> 67.2 us (0.984)
  Pallas kernels: 67.4 us -> 66.2 us
    pallas_call x1, Pallas kernels: 65.1 us -> 64.1 us  [local(): pl.pallas_call(functools.partial(step_kernel, W, N, fold, top, chunk, pie...]
where the time goes in v6:
time: 67.2 us; the launch traced here: 67 us
  Pallas kernels  66.2 us (99%)
  between operations  0.8 us (1%)
    pallas_call x1, Pallas kernels, local(): pl.pallas_call(functools.partial(step_kernel, W, N, fold, top, chunk, pie...  64.1 us
    pallas_call x1, Pallas kernels, local(): pl.pallas_call(functools.partial(store_kernel, fold, top), out_shape=(jax...  2.11 us

profile of v6, /device:TPU:0, one launch (start us, length us, event | category | flops | bytes accessed | tf_op | source)
XLA Modules:
  0.0 67.0 jit_solution(10915539506425630134)
XLA Ops:
  0.6 64.1 %step.1 = (bf16[1024,2048]{1,0:T(8,128)(2,1)S(1)}, f32[32,128]{1,0:T(8,128)S(1)}, s32[64,1024]{1,0:T(8,128)S(1)}) custom-call(s32[64,512]{1,0:T(8,128)} %bitcast.3, f32[1,1024]{1,0:T(1,128)} %bitcast.5, f32[1,2048]{1,0:T(1,128)} %bitcast.4, bf16[512,2048]{1,0:T(8,128)(2,1)} %act_hbm.1, bf16[2048,1024]{1,0:T(8,128)(2,1)} %enc_hbm.1, bf16[1024,2048]{1,0:T(8,128)(2,1)} %dec_hbm.1), custom_call_target="tpu_custom_call" | custom-call | flops 8589934592 | bytes 18874368 | tf_op jit(solution)/shard_map/step/pallas_call | solution.py:562
  64.8 2.1 %store.1 = (bf16[1024,2048]{1,0:T(8,128)(2,1)}, f32[64,1024]{1,0:T(8,128)}) custom-call(bf16[1024,2048]{1,0:T(8,128)(2,1)S(1)} %get-tuple-element.5.dg_ref, f32[32,128]{1,0:T(8,128)S(1)} %get-tuple-element.6.sum_ref, s32[64,1024]{1,0:T(8,128)S(1)} %get-tuple-element.7.slot_ref), custom_call_target="tpu_custom_call" | custom-call | tf_op jit(solution)/shard_map/store/pallas_call | solution.py:600

commit v7 on v6

--- a/solution.py
+++ b/solution.py
@@ -128,7 +128,7 @@
 
     def wide_copy(d, source, target, send, recv):
         return pltpu.make_async_remote_copy(
-            src_ref=source, dst_ref=target, send_sem=send.at[d], recv_sem=recv.at[d],
+            src_ref=source, dst_ref=target, send_sem=send, recv_sem=recv,
             device_id={"wide": mate(d)}, device_id_type=MESH,
         )
 
@@ -144,7 +144,7 @@
         across, along = narrow + 1 - 2 * side, narrow + 2 - 4 * pair
         plain = chunks - early
 
-        PARTS = 2
+        PARTS = 1
         tall = latents // PARTS
 
         def dec_copy(i):
@@ -193,21 +193,24 @@
         return pick(tables, packed_ids(w), fold, top)
 
     def scatter_copy(d, source, target, send, recv):
-        return wide_copy(d, source.at[d], target.at[d], send, recv)
+        return wide_copy(d, source.at[d - 1], target.at[d - 1], send.at[0], recv.at[0])
+
+    def scatter_all(source, target, send, recv):
+        return wide_copy(1, source, target, send.at[0], recv.at[0])
 
     def scatter(first, last, source, target, send, recv):
         picked = None
         for d in range(last - 1, first - 1, -1):
             picked = pick_dense(mate(d))
             if d > 0:
-                source[d] = picked.astype(BF16)
+                source[d - 1] = picked.astype(BF16)
                 scatter_copy(d, source, target, send, recv).start()
         return picked
 
     def gather(picked, source, target, send, recv):
+        scatter_all(source, target, send, recv).wait_recv()
         for d in range(1, W):
-            scatter_copy(d, source, target, send, recv).wait_recv()
-            picked = picked + target[d].astype(F32)
+            picked = picked + target[d - 1].astype(F32)
         return picked
 
     lax.fori_loop(0, pieces, encode_far, 0)
@@ -229,7 +232,11 @@
     values[wide] = gather(summed, part, wide_in, ws1, wr1).astype(BF16)
 
     def value_copy(d):
-        return wide_copy(d, values.at[wide], values.at[wide], ws2, wr2)
+        return wide_copy(d, values.at[wide], values.at[wide], ws2.at[0], wr2.at[d // (W // 2)])
+
+    def values_of(ref, first, last, send, recv):
+        blocks = ref.at[pl.ds(0, last - first)]
+        return wide_copy(1, blocks, blocks, send, recv)
 
     for d in range(W - 1, 0, -1):
         value_copy(d).start()
@@ -248,10 +255,9 @@
             spread = spread_row(table, p, top, latents // LANES, lambda j: slot[at, j * LANES : (j + 1) * LANES])
             lat[at, :] = spread.astype(BF16)
 
-    def fill_mates(first, last):
+    def fill_mates(first, last, group):
+        values_of(values, first, last, ws2.at[0], wr2.at[group]).wait_recv()
         for d in range(first, last):
-            if d > 0:
-                value_copy(d).wait_recv()
             fill_block(mate(d), values, slot, lat)
 
     load_dec.wait()
@@ -296,13 +302,13 @@
 
         def rec_copy(c, q):
             h = near if q == 0 else 1 - near
-            return narrow_copy(across, rec.at[c, h, 1 - side], rec_in.at[c, h], ns1.at[c, q], nr1.at[c, q])
+            return narrow_copy(across, rec.at[c, h, 1 - side], rec_in.at[c, h], ns1.at[0], nr1.at[c])
 
         def msg_copy(c):
-            return narrow_copy(along, msg.at[c], msg_in.at[c], ns2.at[c], nr2.at[c])
+            return narrow_copy(along, msg.at[c], msg_in.at[c], ns2.at[0], nr2.at[c])
 
         def err_copy(c, h):
-            return narrow_copy(across, err_out.at[c, h], err.at[here(h), columns(c)], ns3.at[c, h], nr3.at[c, h])
+            return narrow_copy(across, err_out.at[c, h], err.at[here(h), columns(c)], ns3.at[0], nr3.at[c])
 
         def full_copy(c):
             return narrow_copy(along, full.at[c], full_in.at[c], fs.at[c], fr.at[c])
@@ -318,10 +324,11 @@
                 rec_copy(c, q).start()
             return carry
 
-        fill_mates(0, W // 2)
+        fill_block(wide, values, slot, lat)
+        fill_mates(1, W // 2, 0)
         for c in range(FIRST):
             send_part(c, 0)
-        fill_mates(W // 2, W)
+        fill_mates(W // 2, W, 1)
         for c in range(FIRST):
             send_part(c, 1)
         lax.fori_loop(FIRST, plain, send_rec, 0)
@@ -331,8 +338,7 @@
             return carry
 
         def send_msg(c):
-            for q in range(2):
-                rec_copy(c, q).wait_recv()
+            narrow_copy(across, rec_in.at[c], rec_in.at[c], ns1.at[0], nr1.at[c]).wait_recv()
             msg[c] = (own_use * rec[c, :, side].astype(F32) + mate_use * rec_in[c].astype(F32)).astype(BF16)
             msg_copy(c).start()
 
@@ -363,11 +369,13 @@
             return carry
 
         def values_copies():
-            return [wide_copy(d, values_in.at[wide], values_in.at[wide], vws, vwr) for d in range(1, W)]
+            return [wide_copy(d, values_in.at[wide], values_in.at[wide], vws.at[0], vwr.at[0]) for d in range(1, W)]
+
+        def values_all():
+            return values_of(values_in, 1, W, vws.at[0], vwr.at[0])
 
         def arrive(c):
-            for h in range(2):
-                err_copy(c, h).wait_recv()
+            narrow_copy(across, err_out.at[c], err_out.at[c], ns3.at[0], nr3.at[c]).wait_recv()
 
         def take(c):
             arrive(c)
@@ -387,8 +395,7 @@
             if c < 2:
                 lax.fori_loop((2 + c) * groups // 4, (3 + c) * groups // 4, more_slots, 0)
             if c == 2:
-                for copy in values_copies():
-                    copy.wait_recv()
+                values_all().wait_recv()
                 for block in range(W):
                     fill_block(block, values_in, slot_in, lat_in)
         for i in range(early * PARTS):
@@ -399,24 +406,21 @@
             take(c)
 
 
-        def finish(c, carry):
-            for q in range(2):
-                rec_copy(c, q).wait_send()
-                err_copy(c, q).wait_send()
-            msg_copy(c).wait_send()
-            return carry
-
-        def finish_early():
+        def finish():
+            narrow_copy(across, rec_in, rec_in, ns1.at[0], nr1.at[0]).wait_send()
+            narrow_copy(along, msg, msg, ns2.at[0], nr2.at[0]).wait_send()
+            narrow_copy(across, err_out, err_out, ns3.at[0], nr3.at[0]).wait_send()
             for i in range(early * PARTS):
                 dec_copy(i).wait_send()
             for c in range(early):
                 full_copy(c).wait_send()
             pair_values().wait_send()
-            for copy in values_copies():
-                copy.wait_send()
+            values_all().wait_send()
     else:
         plain = chunks
-        fill_mates(0, W)
+        fill_block(wide, values, slot, lat)
+        fill_mates(1, W // 2, 0)
+        fill_mates(W // 2, W, 1)
         keep_slots()
 
         def goal_of(d):
@@ -465,14 +469,14 @@
             for d in range(1, N):
                 err_copy(c, d).wait_recv()
 
-        def finish(c, carry):
+        def finish_chunk(c, carry):
             for d in range(1, N):
                 rec_copy(c, d).wait_send()
                 err_copy(c, d).wait_send()
             return carry
 
-        def finish_early():
-            pass
+        def finish():
+            lax.fori_loop(0, plain, finish_chunk, 0)
 
     def sent_chunk(c, carry):
         arrive(c)
@@ -493,13 +497,11 @@
     outer(plain - 1)
     sum_ref[...] = gather(summed, lg_packed, grad_in, ws3, wr3)
 
-    for d in range(1, W):
-        scatter_copy(d, part, wide_in, ws1, wr1).wait_send()
-        value_copy(d).wait_send()
-        scatter_copy(d, lg_packed, grad_in, ws3, wr3).wait_send()
-
-    lax.fori_loop(0, plain, finish, 0)
-    finish_early()
+    scatter_all(part, wide_in, ws1, wr1).wait_send()
+    values_of(values, 1, W, ws2.at[0], wr2.at[0]).wait_send()
+    scatter_all(lg_packed, grad_in, ws3, wr3).wait_send()
+
+    finish()
 
 
 STORES = 1
@@ -539,7 +541,7 @@
     early = chunks // 8 if N == 4 else 0
     plain = chunks - early
     half = (plain, 2, tokens // 4, chunk)
-    packed_shape = (W, rows, LANES)
+    packed_shape, mates_shape = (W, rows, LANES), (W - 1, rows, LANES)
     vmem = pl.BlockSpec(memory_space=pltpu.VMEM)
     hbm = pl.BlockSpec(memory_space=pl.ANY)
     dma = pltpu.SemaphoreType.DMA
@@ -553,8 +555,8 @@
             *[pltpu.VMEM(half, BF16)] * 4,
             *[pltpu.VMEM((early, tokens, chunk), BF16)] * 2,
             pltpu.VMEM((early, tokens, chunk), F32),
-            dma((2 * early,)), dma((2 * early,)), dma((1,)), dma((1,)), dma((W,)), dma((W,)),
-            *[dma((plain, 2))] * 2, *[dma((plain,))] * 2, *[dma((plain, 2))] * 2,
+            dma((early,)), dma((early,)), *[dma((1,))] * 4,
+            *[dma((1,)), dma((plain,))] * 3,
             dma((early,)), dma((early,)),
         ]
     else:
@@ -578,16 +580,16 @@
             pltpu.VMEM((latents, channels), BF16),
             pltpu.VMEM((tokens, latents), jnp.int32),
             pltpu.VMEM((tokens, latents), F32),
-            pltpu.VMEM(packed_shape, BF16),
-            pltpu.VMEM(packed_shape, BF16),
+            pltpu.VMEM(mates_shape, BF16),
+            pltpu.VMEM(mates_shape, BF16),
             pltpu.VMEM(packed_shape, BF16),
             pltpu.VMEM((tokens, latents), BF16),
             pltpu.VMEM((latents, tokens), BF16),
             pltpu.VMEM((tokens, channels), BF16),
-            pltpu.VMEM(packed_shape, BF16),
-            pltpu.VMEM(packed_shape, BF16),
+            pltpu.VMEM(mates_shape, BF16),
+            pltpu.VMEM(mates_shape, BF16),
             dma((6 + pieces,)),
-            *[dma((W,))] * 6,
+            dma((1,)), dma((1,)), dma((1,)), dma((2,)), dma((1,)), dma((1,)),
             *scratch,
         ],
         compiler_params=pltpu.CompilerParams(collective_id=0, has_side_effects=True, vmem_limit_bytes=56 * 2**20),

time: 67.2 us -> 66.4 us (0.988)
  Pallas kernels: 66.2 us -> 65.4 us
    pallas_call x1, Pallas kernels: 64.1 us -> 63.3 us  [local(): pl.pallas_call(functools.partial(step_kernel, W, N, fold, top, chunk, pie...]
where the time goes in v7:
time: 66.4 us; the launch traced here: 66.2 us
  Pallas kernels  65.4 us (98%)
  between operations  0.8 us (1%)
    pallas_call x1, Pallas kernels, local(): pl.pallas_call(functools.partial(step_kernel, W, N, fold, top, chunk, pie...  63.3 us
    pallas_call x1, Pallas kernels, local(): pl.pallas_call(functools.partial(store_kernel, fold, top), out_shape=(jax...  2.11 us

profile of v7, /device:TPU:0, one launch (start us, length us, event | category | flops | bytes accessed | tf_op | source)
XLA Modules:
  0.0 66.2 jit_solution(7510949370789268910)
XLA Ops:
  0.6 63.3 %step.1 = (bf16[1024,2048]{1,0:T(8,128)(2,1)S(1)}, f32[32,128]{1,0:T(8,128)S(1)}, s32[64,1024]{1,0:T(8,128)S(1)}) custom-call(s32[64,512]{1,0:T(8,128)} %bitcast.3, f32[1,1024]{1,0:T(1,128)} %bitcast.5, f32[1,2048]{1,0:T(1,128)} %bitcast.4, bf16[512,2048]{1,0:T(8,128)(2,1)} %act_hbm.1, bf16[2048,1024]{1,0:T(8,128)(2,1)} %enc_hbm.1, bf16[1024,2048]{1,0:T(8,128)(2,1)} %dec_hbm.1), custom_call_target="tpu_custom_call" | custom-call | flops 8589934592 | bytes 18874368 | tf_op jit(solution)/shard_map/step/pallas_call | solution.py:564
  63.9 2.1 %store.1 = (bf16[1024,2048]{1,0:T(8,128)(2,1)}, f32[64,1024]{1,0:T(8,128)}) custom-call(bf16[1024,2048]{1,0:T(8,128)(2,1)S(1)} %get-tuple-element.5.dg_ref, f32[32,128]{1,0:T(8,128)S(1)} %get-tuple-element.6.sum_ref, s32[64,1024]{1,0:T(8,128)S(1)} %get-tuple-element.7.slot_ref), custom_call_target="tpu_custom_call" | custom-call | tf_op jit(solution)/shard_map/store/pallas_call | solution.py:602

commit v8 on v7

--- a/solution.py
+++ b/solution.py
@@ -238,7 +238,7 @@
         blocks = ref.at[pl.ds(0, last - first)]
         return wide_copy(1, blocks, blocks, send, recv)
 
-    for d in range(W - 1, 0, -1):
+    for d in (*range(1, W // 2), *range(W - 1, W // 2 - 1, -1)):
         value_copy(d).start()
     if early:
         def pair_values():
@@ -307,8 +307,9 @@
         def msg_copy(c):
             return narrow_copy(along, msg.at[c], msg_in.at[c], ns2.at[0], nr2.at[c])
 
-        def err_copy(c, h):
-            return narrow_copy(across, err_out.at[c, h], err.at[here(h), columns(c)], ns3.at[0], nr3.at[c])
+        def err_copy(c, h, q):
+            at = c + q if c == plain - 1 else c
+            return narrow_copy(across, err_out.at[c, h], err.at[here(h), columns(c)], ns3.at[0], nr3.at[at])
 
         def full_copy(c):
             return narrow_copy(along, full.at[c], full_in.at[c], fs.at[c], fr.at[c])
@@ -344,13 +345,13 @@
 
         def send_err(c):
             msg_copy(c).wait_recv()
-            for h in range(2):
+            for q, h in enumerate((1 - near, near)):
                 shift = shift_ref[:, columns(c)] - act[here(h), columns(c)].astype(F32)
                 mine_rec, mate_rec = rec[c, h, side].astype(F32), rec_in[c, h].astype(F32)
                 other = msg_in[c, h].astype(F32)
                 back = mate_scale * (shift + mate_rec) + least * mine_rec + mate_use * other
                 err_out[c, h] = (back / N).astype(BF16)
-                err_copy(c, h).start()
+                err_copy(c, h, q).start()
                 back = own_scale * (shift + mine_rec) + least * mate_rec + own_use * other
                 err[here(h), columns(c)] = (back / N).astype(BF16)
 
@@ -373,6 +374,10 @@
 
         def values_all():
             return values_of(values_in, 1, W, vws.at[0], vwr.at[0])
+
+        def arrive_last(q):
+            half = err_out.at[plain - 1, 0]
+            narrow_copy(across, half, half, ns3.at[0], nr3.at[plain - 1 + q]).wait_recv()
 
         def arrive(c):
             narrow_copy(across, err_out.at[c], err_out.at[c], ns3.at[0], nr3.at[c]).wait_recv()
@@ -465,6 +470,10 @@
         lax.fori_loop(0, chunks, combine, 0)
         lax.fori_loop(0, latents // LANES, flip, 0)
 
+        def arrive_last(q):
+            if q == 0:
+                arrive(plain - 1)
+
         def arrive(c):
             for d in range(1, N):
                 err_copy(c, d).wait_recv()
@@ -489,9 +498,10 @@
     else:
         total[...] = jnp.zeros_like(total)
         lax.fori_loop(0, plain - 1, sent_chunk, 0)
-    arrive(plain - 1)
+    arrive_last(0)
     total[rows_of(1 - near), :] += contract(plain - 1, rows_of(1 - near))
     scatter(W // 2, W, lg_packed, grad_in, ws3, wr3)
+    arrive_last(1)
     total[rows_of(near), :] += contract(plain - 1, rows_of(near))
     summed = scatter(0, W // 2, lg_packed, grad_in, ws3, wr3)
     outer(plain - 1)
@@ -556,7 +566,7 @@
             *[pltpu.VMEM((early, tokens, chunk), BF16)] * 2,
             pltpu.VMEM((early, tokens, chunk), F32),
             dma((early,)), dma((early,)), *[dma((1,))] * 4,
-            *[dma((1,)), dma((plain,))] * 3,
+            *[dma((1,)), dma((plain,))] * 2, dma((1,)), dma((plain + 1,)),
             dma((early,)), dma((early,)),
         ]
     else:

time: 66.4 us -> 65.4 us (0.985)
  Pallas kernels: 65.4 us -> 64.4 us
    pallas_call x1, Pallas kernels: 63.3 us -> 62.3 us  [local(): pl.pallas_call(functools.partial(step_kernel, W, N, fold, top, chunk, pie...]
where the time goes in v8:
time: 65.4 us; the launch traced here: 65.2 us
  Pallas kernels  64.4 us (98%)
  between operations  0.8 us (1%)
    pallas_call x1, Pallas kernels, local(): pl.pallas_call(functools.partial(step_kernel, W, N, fold, top, chunk, pie...  62.3 us
    pallas_call x1, Pallas kernels, local(): pl.pallas_call(functools.partial(store_kernel, fold, top), out_shape=(jax...  2.11 us

profile of v8, /device:TPU:0, one launch (start us, length us, event | category | flops | bytes accessed | tf_op | source)
XLA Modules:
  0.0 65.2 jit_solution(8168954179103283310)
XLA Ops:
  0.6 62.3 %step.1 = (bf16[1024,2048]{1,0:T(8,128)(2,1)S(1)}, f32[32,128]{1,0:T(8,128)S(1)}, s32[64,1024]{1,0:T(8,128)S(1)}) custom-call(s32[64,512]{1,0:T(8,128)} %bitcast.3, f32[1,1024]{1,0:T(1,128)} %bitcast.5, f32[1,2048]{1,0:T(1,128)} %bitcast.4, bf16[512,2048]{1,0:T(8,128)(2,1)} %act_hbm.1, bf16[2048,1024]{1,0:T(8,128)(2,1)} %enc_hbm.1, bf16[1024,2048]{1,0:T(8,128)(2,1)} %dec_hbm.1), custom_call_target="tpu_custom_call" | custom-call | flops 8589934592 | bytes 18874368 | tf_op jit(solution)/shard_map/step/pallas_call | solution.py:574
  63.0 2.1 %store.1 = (bf16[1024,2048]{1,0:T(8,128)(2,1)}, f32[64,1024]{1,0:T(8,128)}) custom-call(bf16[1024,2048]{1,0:T(8,128)(2,1)S(1)} %get-tuple-element.5.dg_ref, f32[32,128]{1,0:T(8,128)S(1)} %get-tuple-element.6.sum_ref, s32[64,1024]{1,0:T(8,128)S(1)} %get-tuple-element.7.slot_ref), custom_call_target="tpu_custom_call" | custom-call | tf_op jit(solution)/shard_map/store/pallas_call | solution.py:612

commit v9 on v8

--- a/solution.py
+++ b/solution.py
@@ -515,7 +515,7 @@
 
 
 STORES = 1
-AHEAD, HEAD, TURN = 1, 8, 9
+AHEAD, HEAD, TURN = 1, 8, 8
 FIRST, LAG = 3, 3
 
 

time: 65.4 us -> 65.4 us (level)
  no operation moved by 1% of the time
where the time goes in v9:
time: 65.4 us; the launch traced here: 65.3 us
  Pallas kernels  64.5 us (99%)
  between operations  0.8 us (1%)
    pallas_call x1, Pallas kernels, local(): pl.pallas_call(functools.partial(step_kernel, W, N, fold, top, chunk, pie...  62.4 us
    pallas_call x1, Pallas kernels, local(): pl.pallas_call(functools.partial(store_kernel, fold, top), out_shape=(jax...  2.11 us

profile of v9, /device:TPU:0, one launch (start us, length us, event | category | flops | bytes accessed | tf_op | source)
XLA Modules:
  0.0 65.3 jit_solution(1551630991563856524)
XLA Ops:
  0.6 62.4 %step.1 = (bf16[1024,2048]{1,0:T(8,128)(2,1)S(1)}, f32[32,128]{1,0:T(8,128)S(1)}, s32[64,1024]{1,0:T(8,128)S(1)}) custom-call(s32[64,512]{1,0:T(8,128)} %bitcast.3, f32[1,1024]{1,0:T(1,128)} %bitcast.5, f32[1,2048]{1,0:T(1,128)} %bitcast.4, bf16[512,2048]{1,0:T(8,128)(2,1)} %act_hbm.1, bf16[2048,1024]{1,0:T(8,128)(2,1)} %enc_hbm.1, bf16[1024,2048]{1,0:T(8,128)(2,1)} %dec_hbm.1), custom_call_target="tpu_custom_call" | custom-call | flops 8589934592 | bytes 18874368 | tf_op jit(solution)/shard_map/step/pallas_call | solution.py:574
  63.0 2.1 %store.1 = (bf16[1024,2048]{1,0:T(8,128)(2,1)}, f32[64,1024]{1,0:T(8,128)}) custom-call(bf16[1024,2048]{1,0:T(8,128)(2,1)S(1)} %get-tuple-element.5.dg_ref, f32[32,128]{1,0:T(8,128)S(1)} %get-tuple-element.6.sum_ref, s32[64,1024]{1,0:T(8,128)S(1)} %get-tuple-element.7.slot_ref), custom_call_target="tpu_custom_call" | custom-call | tf_op jit(solution)/shard_map/store/pallas_call | solution.py:612
